TPU v7x, 32 devices: a 4x4x1 block of a 4x4x8 slice. The times are simulated.
32 devices in a mesh: dp: 1 (over z), tp: 4 (over y), sp: 8 (over x, core).
Axes of the slice: x: 4, y: 4, z: 1, core: 2. Of those that a mesh axis runs over, the one named last changes fastest.
The devices are a block of a 4x4x8 slice.
Arguments:
- x_in: bfloat16 [131072, 512], P(('dp', 'sp'))
- grad_y: bfloat16 [131072, 512], P(('dp', 'sp'))
- w_qkv: bfloat16 [512, 3, 512], P(None, None, 'tp')
- w_out: bfloat16 [512, 512], P('tp')
- ln_gamma: float32 [512], replicated
- ln_beta: float32 [512], replicated
- temperature: float32 [8], replicated
Outputs:
- output 1: bfloat16 [131072, 512], P(('dp', 'sp'))
- output 2: bfloat16 [131072, 512], P(('dp', 'sp'))
- output 3: float32 [512, 3, 512], P(('dp', 'sp'), None, 'tp')
- output 4: float32 [512, 512], P(('dp', 'tp', 'sp'))
- output 5: float32 [512], P('dp')
- output 6: float32 [512], P('dp')
- output 7: float32 [8], P('dp')
All inputs are finite; a program needn't handle non-finite values.
Results may differ from a plain program's by a relative error of at most 0.001.
Values are sent between devices in bfloat16 or wider.
A program may use at most 768 MiB of HBM per device.

v0:
```python
import jax
import jax.numpy as jnp
from jax import lax
from jax.sharding import PartitionSpec as P

LN_EPS = 1e-6


def layer_norm_fwd(x_rows, ln_gamma, ln_beta):
    x_float = x_rows.astype(jnp.float32)
    centered = x_float - jnp.mean(x_float, axis=-1, keepdims=True)
    inv_std = lax.rsqrt(jnp.mean(centered * centered, axis=-1, keepdims=True) + LN_EPS)
    x_hat = centered * inv_std
    return x_hat, inv_std, (x_hat * ln_gamma + ln_beta).astype(jnp.bfloat16)


def layer_norm_bwd(grad_u, x_hat, inv_std, ln_gamma):
    value_a9 = grad_u * ln_gamma
    return inv_std * (value_a9 - jnp.mean(value_a9, axis=-1, keepdims=True) - x_hat * jnp.mean(value_a9 * x_hat, axis=-1, keepdims=True))


def state_forward(gram_mat, q_sq, k_sq, temp_heads):
    norm_prod = jnp.sqrt(q_sq)[:, :, None] * jnp.sqrt(k_sq)[:, None, :]
    gram_n = gram_mat / norm_prod
    attn_prob = jax.nn.softmax(temp_heads[:, None, None] * gram_n, axis=-1)
    return gram_n, norm_prod, attn_prob


def state_backward(d_attn, attn_prob, gram_n, norm_prod, q_sq, k_sq, temp_heads):
    d_logit = attn_prob * (d_attn - jnp.sum(attn_prob * d_attn, axis=-1, keepdims=True))
    temp_grad = jnp.sum(d_logit * gram_n, axis=(1, 2))
    grad_sn = temp_heads[:, None, None] * d_logit
    d_gram = (grad_sn / norm_prod).astype(jnp.bfloat16)
    prod_sn = grad_sn * gram_n
    q_coef = -jnp.sum(prod_sn, axis=2) / q_sq
    k_coef = -jnp.sum(prod_sn, axis=1) / k_sq
    return d_gram, q_coef, k_coef, temp_grad


def solution(mesh):
    tp_size = mesh.shape["tp"]
    row_spec = P(("dp", "sp"), None)

    def local_step(x_blk, grad_blk, w_qkv, w_out, ln_gamma, ln_beta, value_a11):
        tokens, model_width = x_blk.shape
        local_cols = w_qkv.shape[2]
        heads_loc = value_a11.shape[0] // tp_size
        head_dim = local_cols // heads_loc
        temp_heads = lax.dynamic_slice_in_dim(value_a11, lax.axis_index("tp") * heads_loc, heads_loc)
        x_hat, inv_std, u_act = layer_norm_fwd(x_blk, ln_gamma, ln_beta)
        qkv_act = jnp.einsum("nd,dec->nec", u_act, w_qkv, preferred_element_type=jnp.float32).astype(jnp.bfloat16)
        qkv_heads = qkv_act.reshape(tokens, 3, heads_loc, head_dim)
        q_act = qkv_heads[:, 0]
        k_act = qkv_heads[:, 1]
        v_act = qkv_heads[:, 2]
        gram_part = jnp.einsum("nhi,nhj->hij", q_act, k_act, preferred_element_type=jnp.float32)
        q_part = jnp.einsum("nhi,nhi->hi", q_act, q_act, preferred_element_type=jnp.float32)
        k_part = jnp.einsum("nhj,nhj->hj", k_act, k_act, preferred_element_type=jnp.float32)
        gram_mat, q_sq, k_sq = lax.psum((gram_part, q_part, k_part), "sp")
        gram_n, norm_prod, attn_prob = state_forward(gram_mat, q_sq, k_sq, temp_heads)
        attn_bf = attn_prob.astype(jnp.bfloat16)
        out_act = jnp.einsum("hij,nhj->nhi", attn_bf, v_act, preferred_element_type=jnp.float32).astype(jnp.bfloat16)
        w_out_heads = w_out.reshape(heads_loc, head_dim, model_width)
        y_part = jnp.einsum("nhi,hid->nd", out_act, w_out_heads, preferred_element_type=jnp.float32)
        y_out = (x_blk.astype(jnp.float32) + lax.psum(y_part, "tp")).astype(jnp.bfloat16)
        wout_part = jnp.einsum("nhi,nd->hid", out_act, grad_blk, preferred_element_type=jnp.float32).reshape(local_cols, model_width)
        grad_wout = lax.psum_scatter(wout_part, "sp", scatter_dimension=0, tiled=True)
        dout_act = jnp.einsum("nd,hid->nhi", grad_blk, w_out_heads, preferred_element_type=jnp.float32).astype(jnp.bfloat16)
        d_attn = lax.psum(jnp.einsum("nhi,nhj->hij", dout_act, v_act, preferred_element_type=jnp.float32), "sp")
        dv_act = jnp.einsum("hij,nhi->nhj", attn_bf, dout_act, preferred_element_type=jnp.float32).astype(jnp.bfloat16)
        d_gram, q_coef, k_coef, temp_grad = state_backward(d_attn, attn_prob, gram_n, norm_prod, q_sq, k_sq, temp_heads)
        dq_act = (jnp.einsum("hij,nhj->nhi", d_gram, k_act, preferred_element_type=jnp.float32) + q_act * q_coef).astype(jnp.bfloat16)
        dk_act = (jnp.einsum("hij,nhi->nhj", d_gram, q_act, preferred_element_type=jnp.float32) + k_act * k_coef).astype(jnp.bfloat16)
        dqkv_act = jnp.stack([dq_act, dk_act, dv_act], axis=1).reshape(tokens, 3, local_cols)
        wqkv_part = jnp.einsum("nd,nec->dec", u_act, dqkv_act, preferred_element_type=jnp.float32)
        grad_wqkv = lax.psum_scatter(wqkv_part, "sp", scatter_dimension=0, tiled=True)
        grad_u = lax.psum(jnp.einsum("nec,dec->nd", dqkv_act, w_qkv, preferred_element_type=jnp.float32), "tp")
        grad_gamma, grad_beta = lax.psum((jnp.sum(grad_u * x_hat, axis=0), jnp.sum(grad_u, axis=0)), "sp")
        grad_x = (grad_blk.astype(jnp.float32) + layer_norm_bwd(grad_u, x_hat, inv_std, ln_gamma)).astype(jnp.bfloat16)
        grad_temp = lax.all_gather(temp_grad, "tp", tiled=True)
        return y_out, grad_x, grad_wqkv, grad_wout, grad_gamma, grad_beta, grad_temp

    in_specs = (row_spec, row_spec, P(None, None, "tp"), P("tp", None), P(None), P(None), P(None))
    out_specs = (row_spec, row_spec, P(("dp", "sp"), None, "tp"), P(("dp", "tp", "sp"), None), P("dp"), P("dp"), P("dp"))
    return jax.shard_map(local_step, mesh=mesh, in_specs=in_specs, out_specs=out_specs, check_vma=False)
```

profile of v0, /device:TPU:97, one launch (start us, length us, event | category | flops | bytes accessed | tf_op | source)
XLA Modules:
  0.0 1406.1 jit_solution(107834724081263055)
XLA Ops:
  7.2 0.0 copy-start
  7.2 0.1 all-reduce.7.cloned.1.call-start
  7.3 0.0 copy-start.2
  7.3 7.1 convert_reduce_fusion
  14.4 0.0 copy-start.5
  14.4 3.5 copy-done.2
  17.9 7.2 fusion.16
  25.2 0.2 copy.14
  25.4 20.0 %fusion.73 = f32[16384,384]{0,1} fusion(bf16[512,384]{0,1:T(8,128)(2,1)S(1)} %bitcast.86, bf16[16384,512]{1,0:T(8,128)(2,1)} %param.7, f32[512]{0:T(512)S(1)} %copy-done.11, f32[512]{0:T(512)S(1)} %copy-done.6, f32[16384]{0:T(1024)S(1)} %add_rsqrt_fusion, f32[16384]{0:T(1024)S(1)} %broadcast_multiply_fusion.2), kind=kOutput, calls=%fused_computation.82 | convolution fusion | flops 6492782592 | bytes 42471424
  45.4 10.4 convert_element_type.54
  55.9 4.8 copy-done.3
  60.6 2.5 fusion.29
  63.1 5.3 fusion.31
  68.5 5.5 convolution_convert_fusion.2
  74.0 2.0 copy-done.4
  76.0 4.0 fusion.35
  80.1 0.1 all-reduce.7.cloned.1.call-update
  80.1 0.2 all-reduce.9.cloned.1.call-start
  80.4 0.1 dynamic_slice.3
  80.5 56.3 %all-reduce.7.cloned.1.call-done = (f32[2,64,64]{2,1,0:T(8,128)}, f32[2,64]{1,0:T(2,128)}, f32[2,64]{1,0:T(2,128)}, f32[2,64,64]{2,1,0:T(8,128)}) async-done(((f32[2,64,64]{2,1,0:T(8,128)}, f32[2,64]{1,0:T(2,128)}, f32[2,64]{1,0:T(2,128)}, f32[2,64,64]{2,1,0:T(8,128)}), (f32[2,64,64]{2,1,0:T(8,128)}, f32[2,64]{1,0:T(2,128)}, f32[2,64]{1,0:T(2,128)}, f32[2,64,64]{2,1,0:T(8,128)})) %all-reduce.7.cloned.1.call-update) | async-done | bytes 66576 | tf_op jit(solution)/shard_map/psum | solution.py:59
  136.8 0.6 sqrt.7
  137.4 0.6 sqrt.6
  138.1 1.3 fusion.75
  139.4 5.6 convolution_convert_fusion.1
  145.0 5.6 fusion.22
  150.6 6.4 copy.19
  157.0 0.6 fusion.51
  157.6 7.2 fusion.21
  164.8 7.0 fusion.20
  171.8 6.4 copy.17
  178.2 6.4 copy.18
  184.5 15.5 %convolution_bitcast_fusion.1 = f32[16384,512]{1,0:T(8,128)} fusion(bf16[16384,2,64]{0,2,1:T(8,128)(2,1)} %fusion.22, bf16[2,64,512]{2,1,0:T(8,128)(2,1)S(1)} %bitcast.71), kind=kOutput, calls=%fused_computation.23 | convolution fusion | flops 2147483648 | bytes 37879808 | tf_op jit(solution)/shard_map/nhi,hid->nd/dot_general | solution.py:64
  200.0 18.1 %convolution_bitcast_fusion = f32[16384,512]{1,0:T(8,128)} fusion(bf16[512,3,128]{2,0,1:T(8,128)(2,1)S(1)} %copy-done.5, bf16[16384,1,128]{2,0,1:T(8,128)(2,1)} %copy.19, bf16[16384,1,128]{2,0,1:T(8,128)(2,1)} %copy.18, bf16[16384,1,128]{2,0,1:T(8,128)(2,1)} %copy.17), kind=kOutput, calls=%fused_computation.22 | convolution fusion | flops 6455033856 | bytes 46530560 | tf_op jit(solution)/shard_map/nec,dec->nd/dot_general | solution.py:77
  218.1 0.1 all-reduce.9.cloned.1.call-update
  218.2 0.3 reduce-scatter.5.cloned.1.call-start
  218.5 0.3 copy-done.13
  218.8 0.6 dynamic-slice
  220.0 10.1 fusion.25
  230.1 0.1 reduce-scatter.5.cloned.1.call-update
  230.2 0.1 reduce-scatter.3.cloned.1.call-start
  230.3 0.2 dynamic-update-slice
  230.5 19.2 %fusion.23 = f32[512,3,128]{2,0,1:T(8,128)} fusion(bf16[16384,1,128]{2,0,1:T(8,128)(2,1)} %copy.19, bf16[16384,1,128]{2,0,1:T(8,128)(2,1)} %copy.18, bf16[16384,1,128]{2,0,1:T(8,128)(2,1)} %copy.17, bf16[16384,512]{1,0:T(8,128)(2,1)} %param.7, f32[512]{0:T(512)S(1)} %copy-done.11, f32[512]{0:T(512)S(1)} %copy-done.6, f32[16384]{0:T(1024)S(1)} %add_rsqrt_fusion, ...), kind=kOutput, calls=%fused_computation.34 | convolution fusion | flops 6530531328 | bytes 30281728 | tf_op jit(solution)/shard_map/nd,nec->dec/dot_general | solution.py:75
  249.7 10.4 all-reduce
  260.2 0.1 reduce-scatter.3.cloned.1.call-update
  260.2 1059.5 %all-reduce.9.cloned.1.call-done = (f32[16384,512]{1,0:T(8,128)}, f32[16384,512]{1,0:T(8,128)}) async-done(((f32[16384,512]{1,0:T(8,128)}, f32[16384,512]{1,0:T(8,128)}), (f32[16384,512]{1,0:T(8,128)}, f32[16384,512]{1,0:T(8,128)})) %all-reduce.9.cloned.1.call-update) | async-done | bytes 67108880 | tf_op jit(solution)/shard_map/psum | solution.py:65
  1319.7 22.2 %fusion.15 = (f32[512]{0:T(512)S(1)}, f32[16384]{0:T(1024)S(1)}, f32[16384]{0:T(1024)S(1)}, f32[512]{0:T(512)S(1)}) fusion(f32[16384,512]{1,0:T(8,128)} %get-tuple-element.23, bf16[16384,512]{1,0:T(8,128)(2,1)} %param.7, f32[16384]{0:T(1024)S(1)} %add_rsqrt_fusion, f32[16384]{0:T(1024)S(1)} %broadcast_multiply_fusion.2, f32[512]{0:T(512)S(1)} %copy-done.6), kind=kLoop, calls=%fused_computation.18 | loop fusion | flops 83852288 | bytes 50599936 | tf_op jit(solution)/shard_map/reduce_sum | solution.py:78
  1342.0 44.3 %fusion.14 = (bf16[16384,512]{1,0:T(8,128)(2,1)}, bf16[16384,512]{1,0:T(8,128)(2,1)}) fusion(bf16[16384,512]{1,0:T(8,128)(2,1)} %param.7, bf16[16384,512]{1,0:T(8,128)(2,1)} %param.8, f32[16384,512]{1,0:T(8,128)} %get-tuple-element.23, f32[16384]{0:T(1024)S(1)} %broadcast_multiply_fusion, f32[16384]{0:T(1024)S(1)} %broadcast_multiply_fusion.1, ...), kind=kLoop, calls=%fused_computation.17 | loop fusion | flops 109051904 | bytes 134481920 | tf_op jit(solution)/shard_map/convert_element_type | solution.py:79
  1386.2 13.3 all-reduce.1
  (38 shorter events, 0.1 us)
Async XLA Ops:
  7.2 61.2 %copy-start = (bf16[128,512]{1,0:T(8,128)(2,1)S(1)}, bf16[128,512]{1,0:T(8,128)(2,1)}, u32[]{:S(2)}) copy-start(bf16[128,512]{1,0:T(8,128)(2,1)} %param.10) | copy-start | bytes 393220
  7.2 129.6 %all-reduce.7.cloned.1.call-start = ((), (), s32[]{:S(2)}) async-start(), calls=%async_computation.4 | async-start | bytes 266240 | tf_op jit(solution)/shard_map/psum | solution.py:59
  7.3 10.7 copy-start.2
  14.4 10.8 copy-start.5
  14.4 11.0 copy-start.6
  14.4 11.0 copy-start.11
  45.4 23.0 %slice-start = ((s8[16777216]{0:T(1024)(128)(4,1)}), s8[4194304]{0:T(1024)(128)(4,1)S(1)}, s32[]{:S(2)}) async-start(s8[16777216]{0:T(1024)(128)(4,1)} %bitcast.73), calls=%async_computation.6 | async-start | bytes 8388608
  45.4 23.0 %slice-start.1 = ((s8[16777216]{0:T(1024)(128)(4,1)}), s8[4194304]{0:T(1024)(128)(4,1)S(1)}, s32[]{:S(2)}) async-start(s8[16777216]{0:T(1024)(128)(4,1)} %bitcast.73), calls=%async_computation.7 | async-start | bytes 8388608
  45.4 23.0 %slice-start.2 = ((s8[16777216]{0:T(1024)(128)(4,1)}), s8[4194304]{0:T(1024)(128)(4,1)S(1)}, s32[]{:S(2)}) async-start(s8[16777216]{0:T(1024)(128)(4,1)} %bitcast.73), calls=%async_computation.8 | async-start | bytes 8388608
  55.8 4.8 copy-start.3
  60.6 7.8 slice-start.3
  68.5 11.9 copy-start.12
  74.0 2.0 copy-start.4
  80.1 1239.6 %all-reduce.9.cloned.1.call-start = ((), (), s32[]{:S(2)}) async-start(), calls=%async_computation.5 | async-start | bytes 134217728 | tf_op jit(solution)/shard_map/psum | solution.py:65
  139.4 17.7 %copy-start.9 = (f32[2,64,64]{2,1,0:T(8,128)S(1)}, f32[2,64,64]{2,1,0:T(8,128)}, u32[]{:S(2)}) copy-start(f32[2,64,64]{2,1,0:T(8,128)} %get-tuple-element.18) | copy-start | bytes 98308
  139.4 17.7 %copy-start.10 = (f32[2,64,64]{2,1,0:T(8,128)S(1)}, f32[2,64,64]{2,1,0:T(8,128)}, u32[]{:S(2)}) copy-start(f32[2,64,64]{2,1,0:T(8,128)} %get-tuple-element.21) | copy-start | bytes 98308
  139.4 18.2 %copy-start.7 = (f32[2,64]{1,0:T(2,128)S(1)}, f32[2,64]{1,0:T(2,128)}, u32[]{:S(2)}) copy-start(f32[2,64]{1,0:T(2,128)} %get-tuple-element.19) | copy-start | bytes 1540
  139.4 18.2 %copy-start.8 = (f32[2,64]{1,0:T(2,128)S(1)}, f32[2,64]{1,0:T(2,128)}, u32[]{:S(2)}) copy-start(f32[2,64]{1,0:T(2,128)} %get-tuple-element.20) | copy-start | bytes 1540
  218.1 0.7 copy-start.13
  218.2 1181.4 %reduce-scatter.5.cloned.1.call-start = ((), (), s32[]{:S(2)}) async-start(), calls=%async_computation.3 | async-start | bytes 294912 | tf_op jit(solution)/shard_map/reduce_scatter | solution.py:67
  230.2 1169.4 %reduce-scatter.3.cloned.1.call-start = ((), (), s32[]{:S(2)}) async-start(), calls=%async_computation.2 | async-start | bytes 884736 | tf_op jit(solution)/shard_map/reduce_scatter | solution.py:76
  1341.9 57.6 %copy-start.1 = (bf16[128,512]{1,0:T(8,128)(2,1)S(1)}, bf16[128,512]{1,0:T(8,128)(2,1)}, u32[]{:S(2)}) copy-start(bf16[128,512]{1,0:T(8,128)(2,1)} %param.10) | copy-start | bytes 393220
Sparse Core Ops, SparseCore 0:
  80.2 56.5 all-reduce.6
  218.3 1101.3 all-reduce.8
  1322.5 26.2 reduce-scatter.4
  1351.5 27.8 reduce-scatter.2
where the time goes:
time: 1410 us
  waiting for transfers between devices  1120 us (79%)
  matrix products  123 us (9%)
  other arithmetic  95.6 us (7%)
  local copies, waits for them, and re-layouts  32.1 us (2%)
  blocking collectives  23.7 us (2%)
  between operations  14.7 us (1%)
    psum x1, waiting for transfers between devices, local_step(): lax.psum(y_part, 'tp')  1060 us
    psum x1, waiting for transfers between devices, local_step(): gram_mat, q_sq, k_sq = lax.psum((gram_part, q_part, k_part), 'sp')  56.3 us
    convert_element_type x1, other arithmetic, local_step(): (grad_blk.astype(jnp.float32) + layer_norm_bwd(grad_u, x_hat, inv_std, ln...  44.3 us
  transfers between devices with their start and end apart: 4, of which 2 were waited for; matrix products, arithmetic and copies ran while one was open for 7% of the time, Pallas kernels for 0%

commit v1 on v0

v1 whole, which is shorter than its diff:
```python
import functools

import jax
import jax.numpy as jnp
from jax import lax
from jax.experimental import pallas as pl
from jax.experimental.pallas import tpu as pltpu
from jax.sharding import PartitionSpec as P

LN_EPS = 1e-6
F32 = jnp.float32
BF16 = jnp.bfloat16
MESH = pl.DeviceIdType.MESH
STATS_ROWS = 512
MAIN_ROWS = 512


def dot(lhs, rhs):
    return jnp.dot(lhs, rhs, preferred_element_type=F32)


def dot_rows(lhs, rhs):
    return lax.dot_general(lhs, rhs, (((0,), (0,)), ((), ())), preferred_element_type=F32)


def layer_norm(x, gamma, beta):
    centered = x - jnp.mean(x, axis=-1, keepdims=True)
    inv_std = lax.rsqrt(jnp.mean(centered * centered, axis=-1, keepdims=True) + LN_EPS)
    x_hat = centered * inv_std
    return x_hat, inv_std, (x_hat * gamma + beta).astype(BF16)


def stats_kernel(cols, x_ref, g_ref, w_ref, gamma_ref, beta_ref, qk_ref, dv_ref):
    @pl.when(pl.program_id(0) == 0)
    def _():
        qk_ref[...] = jnp.zeros_like(qk_ref)
        dv_ref[...] = jnp.zeros_like(dv_ref)

    _, _, u = layer_norm(x_ref[...].astype(F32), gamma_ref[...], beta_ref[...])
    qkv = dot(u, w_ref[:, : 3 * cols]).astype(BF16)
    dout = dot(g_ref[...], w_ref[:, 3 * cols :]).astype(BF16)
    qk = qkv[:, : 2 * cols]
    qk_ref[...] += dot_rows(qk, qk)
    dv_ref[...] += dot_rows(dout, qkv[:, 2 * cols :])


def run_stats(x, g, w, gamma, beta):
    tokens, width = x.shape
    cols = w.shape[1] // 4
    rows = STATS_ROWS
    tile = pl.BlockSpec((rows, width), lambda i: (i, 0))
    whole = lambda shape: pl.BlockSpec(shape, lambda i: (0, 0))
    return pl.pallas_call(
        functools.partial(stats_kernel, cols),
        grid=(tokens // rows,),
        out_shape=(
            jax.ShapeDtypeStruct((2 * cols, 2 * cols), F32),
            jax.ShapeDtypeStruct((cols, cols), F32),
        ),
        in_specs=[tile, tile, whole(w.shape), whole((1, width)), whole((1, width))],
        out_specs=(whole((2 * cols, 2 * cols)), whole((cols, cols))),
        compiler_params=pltpu.CompilerParams(dimension_semantics=("arbitrary",), vmem_limit_bytes=40 << 20),
        cost_estimate=pl.CostEstimate(
            flops=2 * tokens * width * 6 * cols, bytes_accessed=4 * tokens * width, transcendentals=0
        ),
        name="stats",
    )(x, g, w, gamma, beta)


def state_kernel(
    n_sp, n_tp, qk_ref, dv_ref, temp_ref, mats_ref, rows_ref, gt_ref,
    gath, mats, rows, sp_send, sp_recv, tp_send, tp_recv,
):
    me_s, me_t = lax.axis_index("sp"), lax.axis_index("tp")
    cols = dv_ref.shape[0]
    hd = cols // 2
    barrier = pltpu.get_barrier_semaphore()
    for d in range(1, n_sp):
        pl.semaphore_signal(barrier, inc=1, device_id={"sp": lax.rem(me_s + d, n_sp)}, device_id_type=MESH)
    for d in range(1, n_tp):
        pl.semaphore_signal(barrier, inc=1, device_id={"tp": lax.rem(me_t + d, n_tp)}, device_id_type=MESH)

    lane = lax.broadcasted_iota(jnp.int32, (hd, cols), 1)
    first = lane < hd
    eye = lax.broadcasted_iota(jnp.int32, (cols, cols), 0) == lax.broadcasted_iota(jnp.int32, (cols, cols), 1)

    def fold(block):
        return jnp.where(first, block[:hd], block[hd:])

    def diag_row(block):
        return jnp.sum(jnp.where(eye, block, 0.0), axis=0, keepdims=True)

    gath[0, :hd] = fold(qk_ref[:cols, cols:])
    gath[0, hd : 2 * hd] = fold(dv_ref[...])
    gath[0, 2 * hd : 2 * hd + 8] = jnp.concatenate(
        [diag_row(qk_ref[:cols, :cols]), diag_row(qk_ref[cols:, cols:]), jnp.zeros((6, cols), F32)], axis=0
    )
    pl.semaphore_wait(barrier, n_sp + n_tp - 2)

    copies = []
    for d in range(1, n_sp):
        copy = pltpu.make_async_remote_copy(
            src_ref=gath.at[0], dst_ref=gath.at[d], send_sem=sp_send.at[d], recv_sem=sp_recv.at[d],
            device_id={"sp": lax.rem(me_s + d, n_sp)}, device_id_type=MESH,
        )
        copy.start()
        copies.append(copy)
    for copy in copies:
        copy.wait()
    total = gath[me_s]
    for s in range(1, n_sp):
        total = total + gath[lax.rem(me_s - s + n_sp, n_sp)]

    gram, d_attn = total[:hd], total[hd : 2 * hd]
    q_row, k_row = total[2 * hd : 2 * hd + 1], total[2 * hd + 1 : 2 * hd + 2]
    q_all = jnp.sum(jnp.where(eye, jnp.broadcast_to(q_row, (cols, cols)), 0.0), axis=1, keepdims=True)
    q_col = jnp.where(first, jnp.broadcast_to(q_all[:hd], (hd, cols)), jnp.broadcast_to(q_all[hd:], (hd, cols)))
    heads = [temp_ref[2 * me_t], temp_ref[2 * me_t + 1]]
    temp = jnp.where(first, heads[0], heads[1])

    def per_head(value, reduce, other):
        lo = reduce(jnp.where(first, value, other), axis=1, keepdims=True)
        hi = reduce(jnp.where(first, other, value), axis=1, keepdims=True)
        return jnp.where(first, jnp.broadcast_to(lo, (hd, cols)), jnp.broadcast_to(hi, (hd, cols)))

    norm = jnp.sqrt(q_col) * jnp.sqrt(k_row)
    gram_n = gram / norm
    logit = temp * gram_n
    expo = jnp.exp(logit - per_head(logit, jnp.max, -jnp.inf))
    attn = expo / per_head(expo, jnp.sum, 0.0)
    d_logit = attn * (d_attn - per_head(attn * d_attn, jnp.sum, 0.0))
    temp_part = jnp.sum(per_head(d_logit * gram_n, jnp.sum, 0.0), axis=0, keepdims=True)
    grad_sn = temp * d_logit
    prod = grad_sn * gram_n
    same = lax.broadcasted_iota(jnp.int32, (hd, cols), 0) == lax.rem(lane, hd)
    q_coef = jnp.sum(jnp.where(same, -per_head(prod, jnp.sum, 0.0) / q_col, 0.0), axis=0, keepdims=True)
    k_coef = -jnp.sum(prod, axis=0, keepdims=True) / k_row

    mats[0, :hd] = attn.astype(BF16)
    mats[0, hd:] = (grad_sn / norm).astype(BF16)
    rows[0] = jnp.concatenate([q_coef, k_coef, temp_part, jnp.zeros((5, cols), F32)], axis=0)
    copies = []
    for d in range(1, n_tp):
        for k, ref in enumerate((mats, rows)):
            copy = pltpu.make_async_remote_copy(
                src_ref=ref.at[0], dst_ref=ref.at[d], send_sem=tp_send.at[k, d], recv_sem=tp_recv.at[k, d],
                device_id={"tp": lax.rem(me_t + d, n_tp)}, device_id_type=MESH,
            )
            copy.start()
            copies.append(copy)
    for copy in copies:
        copy.wait()
    for t in range(n_tp):
        slot = lax.rem(me_t - t + n_tp, n_tp)
        mats_ref[t] = mats[slot]
        part = rows[slot]
        rows_ref[t] = part
        gt_ref[2 * t] = part[2, 0]
        gt_ref[2 * t + 1] = part[2, hd]


def run_state(n_sp, n_tp, qk, dv, temp):
    cols = dv.shape[0]
    n_rows = cols + 8
    vmem = pl.BlockSpec(memory_space=pltpu.VMEM)
    smem = pl.BlockSpec(memory_space=pltpu.SMEM)
    dma = pltpu.SemaphoreType.DMA
    return pl.pallas_call(
        functools.partial(state_kernel, n_sp, n_tp),
        out_shape=(
            jax.ShapeDtypeStruct((n_tp, cols, cols), BF16),
            jax.ShapeDtypeStruct((n_tp, 8, cols), F32),
            jax.ShapeDtypeStruct(temp.shape, F32),
        ),
        in_specs=[vmem, vmem, smem],
        out_specs=(vmem, vmem, smem),
        scratch_shapes=[
            pltpu.VMEM((n_sp, n_rows, cols), F32),
            pltpu.VMEM((n_tp, cols, cols), BF16),
            pltpu.VMEM((n_tp, 8, cols), F32),
            dma((n_sp,)), dma((n_sp,)), dma((2, n_tp)), dma((2, n_tp)),
        ],
        compiler_params=pltpu.CompilerParams(collective_id=0, has_side_effects=True),
        name="state",
    )(qk, dv, temp)


def main_kernel(
    n_tp, t_ref, x_ref, g_ref, w0_ref, w1_ref, w2_ref, w3_ref, mats_ref, rows_ref, gamma_ref, beta_ref,
    y_ref, dx_ref, dw_ref, dwo_ref, dgb_ref,
    w_s, wt_s, wo_s, wot_s, at_s, a_s, gt_s, g_s, co_s, u_s, r_s, o_s, own_s, dwt_s,
):
    width = x_ref.shape[1]
    cols = width // n_tp
    hd = cols // 2
    me_t = t_ref[0]
    step = pl.program_id(0)

    @pl.when(step == 0)
    def _():
        for i, ref in enumerate((w0_ref, w1_ref, w2_ref, w3_ref)):
            at = pl.multiple_of(lax.rem(me_t + i, n_tp) * cols, cols)
            for e in range(3):
                block = ref[:, e * cols : (e + 1) * cols]
                w_s[:, pl.ds(e * width + at, cols)] = block
                wt_s[pl.ds(e * width + at, cols), :] = block.T
            block = ref[:, 3 * cols :]
            wot_s[:, pl.ds(at, cols)] = block
            wo_s[pl.ds(at, cols), :] = block.T
        for ref in (at_s, a_s, gt_s, g_s):
            ref[...] = jnp.zeros_like(ref)
        first = lax.broadcasted_iota(jnp.int32, (hd, cols), 1) < hd
        for t in range(n_tp):
            p, off = t // 2, (t % 2) * cols
            for k, (plain, trans) in enumerate(((a_s, at_s), (g_s, gt_s))):
                block = mats_ref[t, k * hd : (k + 1) * hd].astype(F32)
                full = jnp.concatenate([jnp.where(first, block, 0.0), jnp.where(first, 0.0, block)], axis=0)
                plain[p, off : off + cols, off : off + cols] = full.astype(BF16)
                trans[p, off : off + cols, off : off + cols] = full.T.astype(BF16)
            co_s[0:1, t * cols : (t + 1) * cols] = rows_ref[t, 0:1]
            co_s[1:2, t * cols : (t + 1) * cols] = rows_ref[t, 1:2]
        dwt_s[...] = jnp.zeros_like(dwt_s)
        dwo_ref[...] = jnp.zeros_like(dwo_ref)
        dgb_ref[...] = jnp.zeros_like(dgb_ref)

    gamma = gamma_ref[...]
    x = x_ref[...].astype(F32)
    x_hat, inv_std, u = layer_norm(x, gamma, beta_ref[...])
    u_s[...] = u
    for p in range(2):
        lo, hi = p * 2 * cols, (p + 1) * 2 * cols
        q = dot(u_s[...], w_s[:, lo:hi]).astype(BF16)
        k = dot(u_s[...], w_s[:, width + lo : width + hi]).astype(BF16)
        v = dot(u_s[...], w_s[:, 2 * width + lo : 2 * width + hi]).astype(BF16)
        dout = dot(g_ref[...], wot_s[:, lo:hi]).astype(BF16)
        o_s[:, lo:hi] = dot(v, at_s[p]).astype(BF16)
        r_s[:, 2 * width + lo : 2 * width + hi] = dot(dout, a_s[p]).astype(BF16)
        r_s[:, lo:hi] = (dot(k, gt_s[p]) + q.astype(F32) * co_s[0:1, lo:hi]).astype(BF16)
        r_s[:, width + lo : width + hi] = (dot(q, g_s[p]) + k.astype(F32) * co_s[1:2, lo:hi]).astype(BF16)
    y_ref[...] = (x + dot(o_s[...], wo_s[...])).astype(BF16)
    du = dot(r_s[...], wt_s[...])
    dgb_ref[0:1] += jnp.sum(du * x_hat, axis=0, keepdims=True)
    dgb_ref[1:2] += jnp.sum(du, axis=0, keepdims=True)
    gx = du * gamma
    mean1 = jnp.mean(gx, axis=-1, keepdims=True)
    mean2 = jnp.mean(gx * x_hat, axis=-1, keepdims=True)
    dx_ref[...] = (g_ref[...].astype(F32) + inv_std * (gx - mean1 - x_hat * mean2)).astype(BF16)

    mine = pl.multiple_of(me_t * cols, cols)
    for e in range(3):
        own_s[:, e * cols : (e + 1) * cols] = r_s[:, pl.ds(e * width + mine, cols)]
    dwt_s[...] += dot_rows(own_s[...], u_s[...])
    dwo_ref[...] += dot_rows(o_s[:, pl.ds(mine, cols)], g_ref[...])

    @pl.when(step == pl.num_programs(0) - 1)
    def _():
        for e in range(3):
            dw_ref[:, e * cols : (e + 1) * cols] = dwt_s[e * cols : (e + 1) * cols, :].T


def run_main(n_tp, me_t, x, g, ws, mats, rows, gamma, beta):
    tokens, width = x.shape
    cols = width // n_tp
    r = MAIN_ROWS
    tile = pl.BlockSpec((r, width), lambda i, t: (i, 0))

    def whole(shape):
        return pl.BlockSpec(shape, lambda i, t: (0,) * len(shape))

    vmem = pltpu.VMEM
    pair = (2, 2 * cols, 2 * cols)
    return pl.pallas_call(
        functools.partial(main_kernel, n_tp),
        grid_spec=pltpu.PrefetchScalarGridSpec(
            num_scalar_prefetch=1,
            grid=(tokens // r,),
            in_specs=[tile, tile] + [whole(w.shape) for w in ws]
            + [whole(mats.shape), whole(rows.shape), whole((1, width)), whole((1, width))],
            out_specs=(tile, tile, whole((width, 3 * cols)), whole((cols, width)), whole((8, width))),
            scratch_shapes=[
                vmem((width, 3 * width), BF16), vmem((3 * width, width), BF16),
                vmem((width, width), BF16), vmem((width, width), BF16),
                vmem(pair, BF16), vmem(pair, BF16), vmem(pair, BF16), vmem(pair, BF16),
                vmem((8, width), F32),
                vmem((r, width), BF16), vmem((r, 3 * width), BF16), vmem((r, width), BF16), vmem((r, 3 * cols), BF16),
                vmem((3 * cols, width), F32),
            ],
        ),
        out_shape=(
            jax.ShapeDtypeStruct(x.shape, BF16),
            jax.ShapeDtypeStruct(x.shape, BF16),
            jax.ShapeDtypeStruct((width, 3 * cols), F32),
            jax.ShapeDtypeStruct((cols, width), F32),
            jax.ShapeDtypeStruct((8, width), F32),
        ),
        compiler_params=pltpu.CompilerParams(dimension_semantics=("arbitrary",), vmem_limit_bytes=60 << 20),
        cost_estimate=pl.CostEstimate(
            flops=2 * tokens * width * width * 11, bytes_accessed=8 * tokens * width, transcendentals=0
        ),
        name="main",
    )(me_t, x, g, *ws, mats, rows, gamma, beta)


def reduce_kernel(
    n_chip, dw_ref, dwo_ref, dgb_ref, dw_out, dwo_out, dg_out, db_out,
    got_w, got_o, got_g, sum_w, sum_o, sum_g, in_w, in_o, in_g, a_send, a_recv, b_send, b_recv,
):
    me = lax.axis_index("sp")
    core, chip = lax.rem(me, 2), me // 2
    partner = me + 1 - 2 * core
    barrier = pltpu.get_barrier_semaphore()
    pl.semaphore_signal(barrier, inc=1, device_id={"sp": partner}, device_id_type=MESH)
    peers = [2 * lax.rem(chip + d, n_chip) + core for d in range(n_chip)]
    for d in range(1, n_chip):
        pl.semaphore_signal(barrier, inc=1, device_id={"sp": peers[d]}, device_id_type=MESH)
    pl.semaphore_wait(barrier, n_chip)

    copies = []
    for k, (src, dst) in enumerate(
        ((dw_ref.at[:, 1 - core], got_w), (dwo_ref.at[:, 1 - core], got_o), (dgb_ref, got_g))
    ):
        copy = pltpu.make_async_remote_copy(
            src_ref=src, dst_ref=dst, send_sem=a_send.at[k], recv_sem=a_recv.at[k],
            device_id={"sp": partner}, device_id_type=MESH,
        )
        copy.start()
        copies.append(copy)
    for copy in copies:
        copy.wait()
    sum_w[...] = dw_ref[:, core] + got_w[...]
    sum_o[...] = dwo_ref[:, core] + got_o[...]
    sum_g[...] = dgb_ref[...] + got_g[...]
    in_g[0] = sum_g[...]
    copies = []
    for d in range(1, n_chip):
        to = lax.rem(chip + d, n_chip)
        for k, (src, dst) in enumerate(((sum_w.at[to], in_w.at[d]), (sum_o.at[to], in_o.at[d]), (sum_g, in_g.at[d]))):
            copy = pltpu.make_async_remote_copy(
                src_ref=src, dst_ref=dst, send_sem=b_send.at[k, d], recv_sem=b_recv.at[k, d],
                device_id={"sp": peers[d]}, device_id_type=MESH,
            )
            copy.start()
            copies.append(copy)
    for copy in copies:
        copy.wait()
    w_tot, o_tot, g_tot = sum_w[chip], sum_o[chip], in_g[chip]
    for d in range(1, n_chip):
        w_tot = w_tot + in_w[d]
        o_tot = o_tot + in_o[d]
        g_tot = g_tot + in_g[lax.rem(chip - d + n_chip, n_chip)]
    cols = w_tot.shape[1] // 3
    for e in range(3):
        dw_out[:, e, :] = w_tot[:, e * cols : (e + 1) * cols]
    dwo_out[...] = o_tot
    dg_out[...] = g_tot[0:1]
    db_out[...] = g_tot[1:2]


def run_reduce(n_sp, dw, dwo, dgb):
    width, cols3 = dw.shape
    cols = dwo.shape[0]
    n_chip = n_sp // 2
    dw = dw.reshape(n_chip, 2, width // n_sp, cols3)
    dwo = dwo.reshape(n_chip, 2, cols // n_sp, width)
    w_shape, o_shape, g_shape = (n_chip,) + dw.shape[2:], (n_chip,) + dwo.shape[2:], dgb.shape
    vmem = pl.BlockSpec(memory_space=pltpu.VMEM)
    dma = pltpu.SemaphoreType.DMA
    return pl.pallas_call(
        functools.partial(reduce_kernel, n_chip),
        out_shape=(
            jax.ShapeDtypeStruct((width // n_sp, 3, cols3 // 3), F32),
            jax.ShapeDtypeStruct((cols // n_sp, width), F32),
            jax.ShapeDtypeStruct((1, width), F32),
            jax.ShapeDtypeStruct((1, width), F32),
        ),
        in_specs=[vmem] * 3,
        out_specs=(vmem,) * 4,
        scratch_shapes=[
            pltpu.VMEM(w_shape, F32), pltpu.VMEM(o_shape, F32), pltpu.VMEM(g_shape, F32),
            pltpu.VMEM(w_shape, F32), pltpu.VMEM(o_shape, F32), pltpu.VMEM(g_shape, F32),
            pltpu.VMEM(w_shape, F32), pltpu.VMEM(o_shape, F32), pltpu.VMEM((n_chip,) + g_shape, F32),
            dma((3,)), dma((3,)), dma((3, n_chip)), dma((3, n_chip)),
        ],
        compiler_params=pltpu.CompilerParams(collective_id=1, has_side_effects=True),
        name="reduce",
    )(dw, dwo, dgb)


def solution(mesh):
    n_tp, n_sp = mesh.shape["tp"], mesh.shape["sp"]
    row_spec = P(("dp", "sp"), None)

    def local_step(x, g, w_qkv, w_out, ln_gamma, ln_beta, temperature):
        width = x.shape[1]
        gamma, beta = ln_gamma.reshape(1, width), ln_beta.reshape(1, width)
        me_t = lax.axis_index("tp").astype(jnp.int32).reshape(1)
        w_own = jnp.concatenate([w_qkv.reshape(width, -1), w_out.T], axis=1)
        ws = [w_own]
        for d in range(1, n_tp):
            ws.append(lax.ppermute(w_own, "tp", [((i + d) % n_tp, i) for i in range(n_tp)]))
        qk, dv = run_stats(x, g, w_own, gamma, beta)
        mats, rows, grad_temp = run_state(n_sp, n_tp, qk, dv, temperature)
        y, dx, dw, dwo, dgb = run_main(n_tp, me_t, x, g, ws, mats, rows, gamma, beta)
        dw, dwo, dgamma, dbeta = run_reduce(n_sp, dw, dwo, dgb)
        return y, dx, dw, dwo, dgamma.reshape(-1), dbeta.reshape(-1), grad_temp

    in_specs = (row_spec, row_spec, P(None, None, "tp"), P("tp", None), P(None), P(None), P(None))
    out_specs = (row_spec, row_spec, P(("dp", "sp"), None, "tp"), P(("dp", "tp", "sp"), None), P("dp"), P("dp"), P("dp"))
    return jax.shard_map(local_step, mesh=mesh, in_specs=in_specs, out_specs=out_specs, check_vma=False)
```

time: 1410 us -> 219 us (0.16)
  waiting for transfers between devices: 1120 us -> 0.01 us
  Pallas kernels: 0 us -> 198 us
  matrix products: 123 us -> 0 us
  other arithmetic: 95.6 us -> 0.05 us
  blocking collectives: 23.7 us -> 0 us
  local copies, waits for them, and re-layouts: 32.1 us -> 12.1 us
    psum x2 -> x0, waiting for transfers between devices: 1120 us -> none  [the longest x1 1060 us: local_step(): lax.psum(y_part, 'tp')]
    pallas_call x0 -> x4, Pallas kernels: none -> 198 us  [the longest x1 127 us: run_main(): pl.pallas_call(functools.partial(main_kernel, n_tp), grid_spec=pltpu.Pref...]
    dot_general x11 -> x0, matrix products: 103 us -> none  [the longest x1 19.2 us: local_step(): jnp.einsum('nd,nec->dec', u_act, dqkv_act, preferred_element_type=jnp.flo...]
    convert_element_type x2 -> x0, other arithmetic: 54.7 us -> none  [the longest x1 44.3 us: local_step(): (grad_blk.astype(jnp.float32) + layer_norm_bwd(grad_u, x_hat, inv_std, ln...]
    reduce_sum x3 -> x0, other arithmetic: 36.5 us -> none  [the longest x1 22.2 us: local_step(): jnp.sum(grad_u * x_hat, axis=0)]
    unnamed x1 -> x0, matrix products: 20 us -> none
    another operation x3 -> x0, local copies, waits for them, and re-layouts: 19.1 us -> none  [local_step(): jnp.stack([dq_act, dk_act, dv_act], axis=1).reshape(tokens, 3, local_cols)]
  transfers between devices with their start and end apart: 4 -> 3, of which waited for: 2 -> 0; matrix products, arithmetic and copies ran while one was open for 7% -> 0% of each run, Pallas kernels for 0% -> 26%
where the time goes in v1:
time: 219 us; the launch traced here: 218 us
  Pallas kernels  198 us (90%)
  local copies, waits for them, and re-layouts  12.1 us (6%)
  starting transfers between devices  6.99 us (3%)
    pallas_call x1, Pallas kernels, run_main(): pl.pallas_call(functools.partial(main_kernel, n_tp), grid_spec=pltpu.Pref...  127 us
    pallas_call x1, Pallas kernels, run_stats(): pl.pallas_call(functools.partial(stats_kernel, cols), grid=(tokens // row...  38.1 us
    pallas_call x1, Pallas kernels, run_state(): pl.pallas_call(functools.partial(state_kernel, n_sp, n_tp), out_shape=(ja...  18.6 us
    pallas_call x1, Pallas kernels, run_reduce(): pl.pallas_call(functools.partial(reduce_kernel, n_chip), out_shape=(jax.S...  14.7 us
    unnamed x25, local copies, waits for them, and re-layouts  11.9 us
    ppermute x3, starting transfers between devices, local_step(): lax.ppermute(w_own, 'tp', [((i + d) % n_tp, i) for i in range(n_tp)])  6.99 us
  transfers between devices with their start and end apart: 3, of which 0 were waited for; matrix products, arithmetic and copies ran while one was open for 0% of the time, Pallas kernels for 26%

profile of v1, /device:TPU:97, one launch (start us, length us, event | category | flops | bytes accessed | tf_op | source)
XLA Modules:
  0.0 218.2 jit_solution(1070952481165605852)
XLA Ops:
  0.6 1.0 copy.18
  1.7 1.2 copy.17
  2.8 0.2 copy.19
  3.1 0.0 copy-start
  3.1 2.8 %collective-permute-start.2 = (bf16[512,512]{1,0:T(8,128)(2,1)S(1)}, bf16[512,512]{1,0:T(8,128)(2,1)S(1)}, u32[]{:S(2)}, u32[]{:S(2)}) collective-permute-start(bf16[512,512]{1,0:T(8,128)(2,1)S(1)} %pad_maximum_fusion.w_ref.w0_ref), channel_id=1, source_target_pairs={{24,0},{0,8},{8,16},{16,24},{25,1},{1,9},{9,17},{17,25},{26,2},{2,... | collective-permute-start | bytes 1572872 | tf_op jit(solution)/shard_map/ppermute | solution.py:400
  5.9 3.7 %collective-permute-start.1 = (bf16[512,512]{1,0:T(8,128)(2,1)S(1)}, bf16[512,512]{1,0:T(8,128)(2,1)S(1)}, u32[]{:S(2)}, u32[]{:S(2)}) collective-permute-start(bf16[512,512]{1,0:T(8,128)(2,1)S(1)} %pad_maximum_fusion.w_ref.w0_ref), channel_id=1, source_target_pairs={{16,0},{24,8},{0,16},{8,24},{17,1},{25,9},{1,17},{9,25},{18,2},{26... | collective-permute-start | bytes 1572872 | tf_op jit(solution)/shard_map/ppermute | solution.py:400
  9.6 0.5 collective-permute-start
  10.1 0.0 copy-start.3
  10.1 0.7 copy-done.3
  10.8 0.0 copy-start.4
  10.8 0.7 copy-done.4
  11.5 38.1 %stats.1 = (f32[256,256]{1,0:T(8,128)S(1)}, f32[128,128]{1,0:T(8,128)S(1)}) custom-call(bf16[16384,512]{1,0:T(8,128)(2,1)} %x_ref.3, bf16[16384,512]{1,0:T(8,128)(2,1)} %g_ref.3, bf16[512,512]{1,0:T(8,128)(2,1)S(1)} %pad_maximum_fusion.w_ref.w0_ref, f32[1,512]{1,0:T(1,128)S(1)} %bitcast.10, f32[1,512]{1,0:T(1,128)S(1)} %bitcast.12), custom_call_target="tpu_custom_call" | custom-call | flops 12884901888 | bytes 33554432 | tf_op jit(solution)/shard_map/stats/pallas_call | solution.py:53
  49.5 0.0 copy-done
  49.5 0.0 copy-start.1
  49.6 0.7 copy-done.1
  50.3 0.0 copy-start.2
  50.3 0.6 copy-done.2
  50.9 18.6 %state.1 = (bf16[4,128,128]{2,1,0:T(8,128)(2,1)}, f32[4,8,128]{2,1,0:T(8,128)}, f32[8]{0:T(128)}) custom-call(f32[256,256]{1,0:T(8,128)} %copy-done.1, f32[128,128]{1,0:T(8,128)} %copy-done.2, f32[8]{0:T(128)} %temp_ref.1), custom_call_target="tpu_custom_call" | custom-call | tf_op jit(solution)/shard_map/state/pallas_call | solution.py:168
  69.5 0.0 collective-permute-done.2.w3_ref
  69.5 0.0 copy-start.5
  69.5 0.0 collective-permute-done.1.w2_ref
  69.5 0.0 copy-start.6
  69.6 0.0 collective-permute-done.w1_ref
  69.6 0.0 copy-start.7
  69.6 0.8 copy-done.5
  70.3 0.2 copy-done.6
  70.5 0.2 copy-done.7
  70.7 0.0 copy-start.8
  70.7 126.8 %main.1 = (bf16[16384,512]{1,0:T(8,128)(2,1)}, bf16[16384,512]{1,0:T(8,128)(2,1)}, f32[512,384]{1,0:T(8,128)}, f32[128,512]{1,0:T(8,128)}, f32[8,512]{1,0:T(8,128)}) custom-call(s32[1]{0:T(128)} %bitcast.t_ref, bf16[16384,512]{1,0:T(8,128)(2,1)} %x_ref.3, bf16[16384,512]{1,0:T(8,128)(2,1)} %g_ref.3, bf16[512,512]{1,0:T(8,128)(2,1)} %copy-done, ...), custom_call_target="tpu_custom_call" | custom-call | flops 94489280512 | bytes 67108864 | tf_op jit(solution)/shard_map/main/pallas_call | solution.py:272
  197.5 14.7 %reduce.1 = (f32[64,3,128]{2,1,0:T(4,128)}, f32[16,512]{1,0:T(8,128)}, f32[1,512]{1,0:T(1,128)}, f32[1,512]{1,0:T(1,128)}) custom-call(f32[4,2,64,384]{3,2,1,0:T(8,128)} %bitcast.14, f32[4,2,16,512]{3,2,1,0:T(8,128)} %bitcast.16, f32[8,512]{1,0:T(8,128)} %get-tuple-element.29.dgb_ref), custom_call_target="tpu_custom_call" | custom-call | tf_op jit(solution)/shard_map/reduce/pallas_call | solution.py:368
  212.2 1.6 copy.20
  213.8 1.4 copy.25
  215.2 1.2 copy.26
  216.4 1.3 copy.27
  217.7 0.0 copy-done.8
  217.7 0.5 copy.28
  (1 shorter events, 0.0 us)
Async XLA Ops:
  3.1 46.4 %copy-start = (bf16[512,512]{1,0:T(8,128)(2,1)}, bf16[512,512]{1,0:T(8,128)(2,1)S(1)}, u32[]{:S(2)}) copy-start(bf16[512,512]{1,0:T(8,128)(2,1)S(1)} %pad_maximum_fusion.w_ref.w0_ref) | copy-start | bytes 1572868
  3.1 66.4 %collective-permute-start.2 = (bf16[512,512]{1,0:T(8,128)(2,1)S(1)}, bf16[512,512]{1,0:T(8,128)(2,1)S(1)}, u32[]{:S(2)}, u32[]{:S(2)}) collective-permute-start(bf16[512,512]{1,0:T(8,128)(2,1)S(1)} %pad_maximum_fusion.w_ref.w0_ref), channel_id=1, source_target_pairs={{24,0},{0,8},{8,16},{16,24},{25,1},{1,9},{9,17},{17,25},{26,2},{2,... | collective-permute-start | bytes 1572872 | tf_op jit(solution)/shard_map/ppermute | solution.py:400
  5.9 63.7 %collective-permute-start.1 = (bf16[512,512]{1,0:T(8,128)(2,1)S(1)}, bf16[512,512]{1,0:T(8,128)(2,1)S(1)}, u32[]{:S(2)}, u32[]{:S(2)}) collective-permute-start(bf16[512,512]{1,0:T(8,128)(2,1)S(1)} %pad_maximum_fusion.w_ref.w0_ref), channel_id=1, source_target_pairs={{16,0},{24,8},{0,16},{8,24},{17,1},{25,9},{1,17},{9,25},{18,2},{26... | collective-permute-start | bytes 1572872 | tf_op jit(solution)/shard_map/ppermute | solution.py:400
  9.6 60.0 %collective-permute-start = (bf16[512,512]{1,0:T(8,128)(2,1)S(1)}, bf16[512,512]{1,0:T(8,128)(2,1)S(1)}, u32[]{:S(2)}, u32[]{:S(2)}) collective-permute-start(bf16[512,512]{1,0:T(8,128)(2,1)S(1)} %pad_maximum_fusion.w_ref.w0_ref), channel_id=1, source_target_pairs={{8,0},{16,8},{24,16},{0,24},{9,1},{17,9},{25,17},{1,25},{10,2},{18... | collective-permute-start | bytes 1572872 | tf_op jit(solution)/shard_map/ppermute | solution.py:400
  10.1 0.7 copy-start.3
  10.8 0.7 copy-start.4
  49.5 0.7 copy-start.1
  50.3 0.6 copy-start.2
  69.5 0.8 copy-start.5
  69.5 1.0 copy-start.6
  69.6 1.1 copy-start.7
  70.7 147.0 %copy-start.8 = (f32[8]{0:T(128)S(1)}, f32[8]{0:T(128)}, u32[]{:S(2)}) copy-start(f32[8]{0:T(128)} %get-tuple-element.62) | copy-start | bytes 100

commit v2 on v0

v2 whole, which is shorter than its diff:
```python
import functools

import jax
import jax.numpy as jnp
from jax import lax
from jax.experimental import pallas as pl
from jax.experimental.pallas import tpu as pltpu
from jax.sharding import PartitionSpec as P

LN_EPS = 1e-6
F32 = jnp.float32
BF16 = jnp.bfloat16
MESH = pl.DeviceIdType.MESH
STATS_ROWS = 2048
STATS_SUB = 512
MAIN_ROWS = 2048
MAIN_SUB = 512


def dot(lhs, rhs):
    return jnp.dot(lhs, rhs, preferred_element_type=F32)


def dot_rows(lhs, rhs):
    return lax.dot_general(lhs, rhs, (((0,), (0,)), ((), ())), preferred_element_type=F32)


def layer_norm(x, gamma, beta):
    centered = x - jnp.mean(x, axis=-1, keepdims=True)
    inv_std = lax.rsqrt(jnp.mean(centered * centered, axis=-1, keepdims=True) + LN_EPS)
    x_hat = centered * inv_std
    return x_hat, inv_std, (x_hat * gamma + beta).astype(BF16)


def state_kernel(
    n_sp, n_tp, x_ref, g_ref, w_ref, wo_ref, gamma_ref, beta_ref, temp_ref, w_any, wo_any,
    w_all, wo_all, mats_ref, rows_ref, gt_ref,
    w_s, u_s, qk_s, dv_s, pair, gath, mats, rows,
    w_send, w_recv, w_local, pair_send, pair_recv, sp_send, sp_recv, tp_send, tp_recv,
):
    step = pl.program_id(0)
    me_s, me_t = lax.axis_index("sp"), lax.axis_index("tp")
    n_chip = n_sp // 2
    core, chip = lax.rem(me_s, 2), me_s // 2
    cols, width = wo_ref.shape
    hd = cols // 2
    partner = {"sp": me_s + 1 - 2 * core}
    chips = [{"sp": 2 * lax.rem(chip + d, n_chip) + core} for d in range(n_chip)]
    tps = [{"tp": lax.rem(me_t + d, n_tp)} for d in range(n_tp)]

    def weight_copies():
        for d in range(1, n_tp):
            for k, (src, dst) in enumerate(((w_any, w_all), (wo_any, wo_all))):
                yield pltpu.make_async_remote_copy(
                    src_ref=src, dst_ref=dst.at[me_t], send_sem=w_send.at[k, d], recv_sem=w_recv.at[k, d],
                    device_id=tps[d], device_id_type=MESH,
                )
        for k, (src, dst) in enumerate(((w_any, w_all), (wo_any, wo_all))):
            yield pltpu.make_async_copy(src, dst.at[me_t], w_local.at[k])

    @pl.when(step == 0)
    def _():
        barrier = pltpu.get_barrier_semaphore()
        for peer in [partner] + chips[1:] + tps[1:]:
            pl.semaphore_signal(barrier, inc=1, device_id=peer, device_id_type=MESH)
        pl.semaphore_wait(barrier, n_chip + n_tp - 1)
        for copy in weight_copies():
            copy.start()
        for e in range(3):
            w_s[:, e * cols : (e + 1) * cols] = w_ref[e]
        w_s[:, 3 * cols :] = wo_ref[...].T
        qk_s[...] = jnp.zeros_like(qk_s)
        dv_s[...] = jnp.zeros_like(dv_s)

    sub = u_s.shape[1]
    n_sub = x_ref.shape[0] // sub
    gamma, beta = gamma_ref[...], beta_ref[...]

    def norm(s):
        u_s[s % 2] = layer_norm(x_ref[s * sub : (s + 1) * sub].astype(F32), gamma, beta)[2]

    def sums(s):
        u = u_s[s % 2]
        qk = dot(u, w_s[:, : 2 * cols]).astype(BF16)
        v = dot(u, w_s[:, 2 * cols : 3 * cols]).astype(BF16)
        dout = dot(g_ref[s * sub : (s + 1) * sub], w_s[:, 3 * cols :]).astype(BF16)
        qk_s[...] += dot_rows(qk, qk)
        dv_s[...] += dot_rows(dout, v)

    norm(0)
    for s in range(n_sub):
        if s + 1 < n_sub:
            norm(s + 1)
        sums(s)

    @pl.when(step == pl.num_programs(0) - 1)
    def _():
        lane = lax.broadcasted_iota(jnp.int32, (hd, cols), 1)
        first = lane < hd
        eye = lax.broadcasted_iota(jnp.int32, (cols, cols), 0) == lax.broadcasted_iota(jnp.int32, (cols, cols), 1)

        def fold(block):
            return jnp.where(first, block[:hd], block[hd:])

        def diag_row(block):
            return jnp.sum(jnp.where(eye, block, 0.0), axis=0, keepdims=True)

        pair[0, :hd] = fold(qk_s[:cols, cols:])
        pair[0, hd : 2 * hd] = fold(dv_s[...])
        pair[0, 2 * hd :] = jnp.concatenate(
            [diag_row(qk_s[:cols, :cols]), diag_row(qk_s[cols:, cols:]), jnp.zeros((6, cols), F32)], axis=0
        )
        copy = pltpu.make_async_remote_copy(
            src_ref=pair.at[0], dst_ref=pair.at[1], send_sem=pair_send, recv_sem=pair_recv,
            device_id=partner, device_id_type=MESH,
        )
        copy.start()
        copy.wait()
        gath[0] = pair[0] + pair[1]
        copies = []
        for d in range(1, n_chip):
            copy = pltpu.make_async_remote_copy(
                src_ref=gath.at[0], dst_ref=gath.at[d], send_sem=sp_send.at[d], recv_sem=sp_recv.at[d],
                device_id=chips[d], device_id_type=MESH,
            )
            copy.start()
            copies.append(copy)
        for copy in copies:
            copy.wait()
        total = gath[chip]
        for c in range(1, n_chip):
            total = total + gath[lax.rem(chip - c + n_chip, n_chip)]

        gram, d_attn = total[:hd], total[hd : 2 * hd]
        q_row, k_row = total[2 * hd : 2 * hd + 1], total[2 * hd + 1 : 2 * hd + 2]
        q_all = jnp.sum(jnp.where(eye, jnp.broadcast_to(q_row, (cols, cols)), 0.0), axis=1, keepdims=True)
        q_col = jnp.where(first, jnp.broadcast_to(q_all[:hd], (hd, cols)), jnp.broadcast_to(q_all[hd:], (hd, cols)))
        temp = jnp.where(first, temp_ref[2 * me_t], temp_ref[2 * me_t + 1])

        def per_head(value, reduce, other):
            lo = reduce(jnp.where(first, value, other), axis=1, keepdims=True)
            hi = reduce(jnp.where(first, other, value), axis=1, keepdims=True)
            return jnp.where(first, jnp.broadcast_to(lo, (hd, cols)), jnp.broadcast_to(hi, (hd, cols)))

        norm_prod = jnp.sqrt(q_col) * jnp.sqrt(k_row)
        gram_n = gram / norm_prod
        logit = temp * gram_n
        expo = jnp.exp(logit - per_head(logit, jnp.max, -jnp.inf))
        attn = expo / per_head(expo, jnp.sum, 0.0)
        d_logit = attn * (d_attn - per_head(attn * d_attn, jnp.sum, 0.0))
        temp_part = jnp.sum(per_head(d_logit * gram_n, jnp.sum, 0.0), axis=0, keepdims=True)
        grad_sn = temp * d_logit
        prod = grad_sn * gram_n
        same = lax.broadcasted_iota(jnp.int32, (hd, cols), 0) == lax.rem(lane, hd)
        q_coef = jnp.sum(jnp.where(same, -per_head(prod, jnp.sum, 0.0) / q_col, 0.0), axis=0, keepdims=True)
        k_coef = -jnp.sum(prod, axis=0, keepdims=True) / k_row

        mats[0, :hd] = attn.astype(BF16)
        mats[0, hd:] = (grad_sn / norm_prod).astype(BF16)
        rows[0] = jnp.concatenate([q_coef, k_coef, temp_part, jnp.zeros((5, cols), F32)], axis=0)
        copies = []
        for d in range(1, n_tp):
            for k, ref in enumerate((mats, rows)):
                copy = pltpu.make_async_remote_copy(
                    src_ref=ref.at[0], dst_ref=ref.at[d], send_sem=tp_send.at[k, d], recv_sem=tp_recv.at[k, d],
                    device_id=tps[d], device_id_type=MESH,
                )
                copy.start()
                copies.append(copy)
        for copy in copies:
            copy.wait()
        for t in range(n_tp):
            slot = lax.rem(me_t - t + n_tp, n_tp)
            mats_ref[t] = mats[slot]
            part = rows[slot]
            rows_ref[t] = part
            gt_ref[2 * t] = part[2, 0]
            gt_ref[2 * t + 1] = part[2, hd]
        for copy in weight_copies():
            copy.wait()


def run_state(n_sp, n_tp, x, g, w, wo, gamma, beta, temp):
    tokens, width = x.shape
    cols = wo.shape[0]
    r, sub = STATS_ROWS, STATS_SUB
    tile = pl.BlockSpec((r, width), lambda i: (i, 0))

    def whole(shape):
        return pl.BlockSpec(shape, lambda i: (0,) * len(shape))

    hbm = pl.BlockSpec(memory_space=pl.ANY)
    smem = pl.BlockSpec(memory_space=pltpu.SMEM)
    vmem, dma = pltpu.VMEM, pltpu.SemaphoreType.DMA
    return pl.pallas_call(
        functools.partial(state_kernel, n_sp, n_tp),
        grid=(tokens // r,),
        out_shape=(
            jax.ShapeDtypeStruct((n_tp,) + w.shape, BF16),
            jax.ShapeDtypeStruct((n_tp,) + wo.shape, BF16),
            jax.ShapeDtypeStruct((n_tp, cols, cols), BF16),
            jax.ShapeDtypeStruct((n_tp, 8, cols), F32),
            jax.ShapeDtypeStruct(temp.shape, F32),
        ),
        in_specs=[tile, tile, whole(w.shape), whole(wo.shape), whole((1, width)), whole((1, width)), smem, hbm, hbm],
        out_specs=(hbm, hbm, whole((n_tp, cols, cols)), whole((n_tp, 8, cols)), smem),
        scratch_shapes=[
            vmem((width, 4 * cols), BF16), vmem((2, sub, width), BF16),
            vmem((2 * cols, 2 * cols), F32), vmem((cols, cols), F32),
            vmem((2, cols + 8, cols), F32), vmem((n_sp // 2, cols + 8, cols), F32),
            vmem((n_tp, cols, cols), BF16), vmem((n_tp, 8, cols), F32),
            dma((2, n_tp)), dma((2, n_tp)), dma((2,)), dma, dma, dma((n_sp // 2,)), dma((n_sp // 2,)),
            dma((2, n_tp)), dma((2, n_tp)),
        ],
        compiler_params=pltpu.CompilerParams(
            dimension_semantics=("arbitrary",), vmem_limit_bytes=48 << 20, collective_id=0, has_side_effects=True
        ),
        name="state",
    )(x, g, w, wo, gamma, beta, temp, w, wo)


def main_kernel(
    n_tp, t_ref, x_ref, g_ref, w_ref, wo_ref, mats_ref, rows_ref, gamma_ref, beta_ref,
    y_ref, dx_ref, dw_ref, dwo_ref, dgb_ref,
    w_s, wt_s, wo_s, wot_s, at_s, a_s, gt_s, g_s, co_s, u_s, r_s, o_s, own_s, xh_s, du_s, dwt_s,
):
    width = x_ref.shape[1]
    cols = width // n_tp
    hd = cols // 2
    me_t = t_ref[0]
    step = pl.program_id(0)

    @pl.when(step == 0)
    def _():
        for t in range(n_tp):
            at = t * cols
            for e in range(3):
                w_s[:, e * width + at : e * width + at + cols] = w_ref[t, e]
                wt_s[e * width + at : e * width + at + cols, :] = w_ref[t, e].T
            wo_s[at : at + cols, :] = wo_ref[t]
            wot_s[:, at : at + cols] = wo_ref[t].T
        for ref in (at_s, a_s, gt_s, g_s):
            ref[...] = jnp.zeros_like(ref)
        first = lax.broadcasted_iota(jnp.int32, (hd, cols), 1) < hd
        for t in range(n_tp):
            p, off = t // 2, (t % 2) * cols
            for k, (plain, trans) in enumerate(((a_s, at_s), (g_s, gt_s))):
                block = mats_ref[t, k * hd : (k + 1) * hd].astype(F32)
                full = jnp.concatenate([jnp.where(first, block, 0.0), jnp.where(first, 0.0, block)], axis=0)
                plain[p, off : off + cols, off : off + cols] = full.astype(BF16)
                trans[p, off : off + cols, off : off + cols] = full.T.astype(BF16)
            co_s[0:1, t * cols : (t + 1) * cols] = rows_ref[t, 0:1]
            co_s[1:2, t * cols : (t + 1) * cols] = rows_ref[t, 1:2]
        dwt_s[...] = jnp.zeros_like(dwt_s)
        dwo_ref[...] = jnp.zeros_like(dwo_ref)
        dgb_ref[...] = jnp.zeros_like(dgb_ref)

    sub = u_s.shape[1]
    n_sub = x_ref.shape[0] // sub
    gamma, beta = gamma_ref[...], beta_ref[...]
    mine = pl.multiple_of(me_t * cols, cols)

    def norm(s):
        x_hat, inv_std, u = layer_norm(x_ref[s * sub : (s + 1) * sub].astype(F32), gamma, beta)
        xh_s[s % 2] = x_hat
        u_s[s % 2] = u
        return inv_std

    def attend(s):
        b, at = s % 2, slice(s * sub, (s + 1) * sub)
        for p in range(2):
            lo, hi = p * 2 * cols, (p + 1) * 2 * cols
            q = dot(u_s[b], w_s[:, lo:hi]).astype(BF16)
            k = dot(u_s[b], w_s[:, width + lo : width + hi]).astype(BF16)
            v = dot(u_s[b], w_s[:, 2 * width + lo : 2 * width + hi]).astype(BF16)
            dout = dot(g_ref[at], wot_s[:, lo:hi]).astype(BF16)
            o_s[b, :, lo:hi] = dot(v, at_s[p]).astype(BF16)
            r_s[b, :, 2 * width + lo : 2 * width + hi] = dot(dout, a_s[p]).astype(BF16)
            r_s[b, :, lo:hi] = (dot(k, gt_s[p]) + q.astype(F32) * co_s[0:1, lo:hi]).astype(BF16)
            r_s[b, :, width + lo : width + hi] = (dot(q, g_s[p]) + k.astype(F32) * co_s[1:2, lo:hi]).astype(BF16)
        y_ref[at] = (x_ref[at].astype(F32) + dot(o_s[b], wo_s[...])).astype(BF16)
        du_s[b] = dot(r_s[b], wt_s[...])

    def weights(s):
        b, at = s % 2, slice(s * sub, (s + 1) * sub)
        for e in range(3):
            own_s[b, :, e * cols : (e + 1) * cols] = r_s[b, :, pl.ds(e * width + mine, cols)]
        dwt_s[...] += dot_rows(own_s[b], u_s[b])
        dwo_ref[...] += dot_rows(o_s[b, :, pl.ds(mine, cols)], g_ref[at])

    def norm_grad(s, inv_std):
        b, at = s % 2, slice(s * sub, (s + 1) * sub)
        du, x_hat = du_s[b], xh_s[b]
        dgb_ref[0:1] += jnp.sum(du * x_hat, axis=0, keepdims=True)
        dgb_ref[1:2] += jnp.sum(du, axis=0, keepdims=True)
        gx = du * gamma
        mean1 = jnp.mean(gx, axis=-1, keepdims=True)
        mean2 = jnp.mean(gx * x_hat, axis=-1, keepdims=True)
        dx_ref[at] = (g_ref[at].astype(F32) + inv_std * (gx - mean1 - x_hat * mean2)).astype(BF16)

    inv = {0: norm(0)}
    for s in range(n_sub):
        if s + 1 < n_sub:
            inv[s + 1] = norm(s + 1)
        attend(s)
        norm_grad(s, inv[s])
        weights(s)

    @pl.when(step == pl.num_programs(0) - 1)
    def _():
        for e in range(3):
            dw_ref[:, e * cols : (e + 1) * cols] = dwt_s[e * cols : (e + 1) * cols, :].T


def run_main(n_tp, me_t, x, g, w, wo, mats, rows, gamma, beta):
    tokens, width = x.shape
    cols = width // n_tp
    r, sub = MAIN_ROWS, MAIN_SUB
    tile = pl.BlockSpec((r, width), lambda i, t: (i, 0))

    def whole(shape):
        return pl.BlockSpec(shape, lambda i, t: (0,) * len(shape))

    vmem = pltpu.VMEM
    pair = (2, 2 * cols, 2 * cols)
    return pl.pallas_call(
        functools.partial(main_kernel, n_tp),
        grid_spec=pltpu.PrefetchScalarGridSpec(
            num_scalar_prefetch=1,
            grid=(tokens // r,),
            in_specs=[tile, tile] + [whole(a.shape) for a in (w, wo, mats, rows, gamma, beta)],
            out_specs=(tile, tile, whole((width, 3 * cols)), whole((cols, width)), whole((8, width))),
            scratch_shapes=[
                vmem((width, 3 * width), BF16), vmem((3 * width, width), BF16),
                vmem((width, width), BF16), vmem((width, width), BF16),
                vmem(pair, BF16), vmem(pair, BF16), vmem(pair, BF16), vmem(pair, BF16),
                vmem((8, width), F32),
                vmem((2, sub, width), BF16), vmem((2, sub, 3 * width), BF16),
                vmem((2, sub, width), BF16), vmem((2, sub, 3 * cols), BF16),
                vmem((2, sub, width), F32), vmem((2, sub, width), F32),
                vmem((3 * cols, width), F32),
            ],
        ),
        out_shape=(
            jax.ShapeDtypeStruct(x.shape, BF16),
            jax.ShapeDtypeStruct(x.shape, BF16),
            jax.ShapeDtypeStruct((width, 3 * cols), F32),
            jax.ShapeDtypeStruct((cols, width), F32),
            jax.ShapeDtypeStruct((8, width), F32),
        ),
        compiler_params=pltpu.CompilerParams(dimension_semantics=("arbitrary",), vmem_limit_bytes=60 << 20),
        cost_estimate=pl.CostEstimate(
            flops=2 * tokens * width * width * 11, bytes_accessed=8 * tokens * width, transcendentals=0
        ),
        name="main",
    )(me_t, x, g, w, wo, mats, rows, gamma, beta)


def reduce_kernel(
    n_chip, dw_ref, dwo_ref, dgb_ref, dw_out, dwo_out, g_out,
    got_w, got_o, sum_w, sum_o, via_w, via_o, in_w, in_o, gam, in_g,
    a_send, a_recv, g_send, g_recv, b_send, b_recv,
):
    me = lax.axis_index("sp")
    core, chip = lax.rem(me, 2), me // 2
    partner = {"sp": me + 1 - 2 * core}
    right, far, left = (lax.rem(chip + d, n_chip) for d in range(1, n_chip))
    peers = [None] + [{"sp": 2 * c + core} for c in (right, far, left)]
    barrier = pltpu.get_barrier_semaphore()
    for peer in [partner] + peers[1:]:
        pl.semaphore_signal(barrier, inc=1, device_id=peer, device_id_type=MESH)
    for c in range(4):
        gam[0, c : c + 1] = dgb_ref[0:1, c * 128 : (c + 1) * 128]
        gam[0, 4 + c : 5 + c] = dgb_ref[1:2, c * 128 : (c + 1) * 128]
    pl.semaphore_wait(barrier, n_chip)

    def remote(src, dst, send, recv, peer):
        copy = pltpu.make_async_remote_copy(
            src_ref=src, dst_ref=dst, send_sem=send, recv_sem=recv, device_id=peer, device_id_type=MESH
        )
        copy.start()
        return copy

    w_copy = remote(dw_ref.at[:, 1 - core], got_w, a_send.at[0], a_recv.at[0], partner)
    o_copy = remote(dwo_ref.at[:, 1 - core], got_o, a_send.at[1], a_recv.at[1], partner)
    g_copy = remote(gam.at[0], gam.at[1], a_send.at[2], a_recv.at[2], partner)
    w_copy.wait()
    o_copy.wait()
    sum_w[...] = dw_ref[:, core] + got_w[...]
    sum_o[...] = dwo_ref[:, core] + got_o[...]
    hw, ho = sum_w.shape[1] // 2, sum_o.shape[1] // 2
    w_half, o_half = (pl.ds(0, hw), pl.ds(hw, hw)), (pl.ds(0, ho), pl.ds(ho, ho))

    via, near, last = [], [], []
    for h, peer in ((0, peers[1]), (1, peers[3])):
        via.append(remote(sum_w.at[far, w_half[h]], via_w.at[h], b_send.at[0, h], b_recv.at[0, h], peer))
        via.append(remote(sum_o.at[far, o_half[h]], via_o.at[h], b_send.at[1, h], b_recv.at[1, h], peer))
    for h, to, peer in ((0, right, peers[1]), (1, left, peers[3])):
        o = 1 - h
        near.append(remote(sum_w.at[to, w_half[o]], in_w.at[h, w_half[o]], b_send.at[2, h], b_recv.at[2, h], peer))
        near.append(remote(sum_o.at[to, o_half[o]], in_o.at[h, o_half[o]], b_send.at[3, h], b_recv.at[3, h], peer))
    g_copy.wait()
    in_g[0] = gam[0] + gam[1]
    for d in range(1, n_chip):
        near.append(remote(in_g.at[0], in_g.at[d], g_send.at[d], g_recv.at[d], peers[d]))
    for h, to, peer in ((0, right, peers[1]), (1, left, peers[3])):
        via[2 * h].wait()
        via[2 * h + 1].wait()
        sum_w[to, w_half[h]] += via_w[h]
        sum_o[to, o_half[h]] += via_o[h]
        last.append(remote(sum_w.at[to, w_half[h]], in_w.at[h, w_half[h]], b_send.at[4, h], b_recv.at[4, h], peer))
        last.append(remote(sum_o.at[to, o_half[h]], in_o.at[h, o_half[h]], b_send.at[5, h], b_recv.at[5, h], peer))
    for copy in near + last:
        copy.wait()
    w_tot = sum_w[chip] + in_w[0] + in_w[1]
    cols = dw_out.shape[2]
    for e in range(3):
        dw_out[e] = w_tot[:, e * cols : (e + 1) * cols]
    dwo_out[...] = sum_o[chip] + in_o[0] + in_o[1]
    g_tot = in_g[chip]
    for c in range(1, n_chip):
        g_tot = g_tot + in_g[lax.rem(chip - c + n_chip, n_chip)]
    g_out[...] = g_tot


def finish_kernel(dw_ref, dwo_ref, g_ref, gt_ref, dw_out, dwo_out, dg_out, db_out, gt_out):
    dw_out[...] = dw_ref[...]
    dwo_out[...] = dwo_ref[...]
    for c in range(4):
        dg_out[0:1, c * 128 : (c + 1) * 128] = g_ref[c : c + 1]
        db_out[0:1, c * 128 : (c + 1) * 128] = g_ref[4 + c : 5 + c]
    for h in range(gt_ref.shape[0]):
        gt_out[h] = gt_ref[h]


def run_reduce(n_sp, dw, dwo, dgb, grad_temp):
    width, cols3 = dw.shape
    cols = dwo.shape[0]
    n_chip = n_sp // 2
    assert n_chip == 4 and width == 512
    dw = dw.reshape(n_chip, 2, width // n_sp, cols3)
    dwo = dwo.reshape(n_chip, 2, cols // n_sp, width)
    w_shape, o_shape = dw.shape[2:], dwo.shape[2:]
    w_half, o_half = (w_shape[0] // 2, w_shape[1]), (o_shape[0] // 2, o_shape[1])
    spec = pl.BlockSpec(memory_space=pltpu.VMEM)
    smem = pl.BlockSpec(memory_space=pltpu.SMEM)
    vmem, dma = pltpu.VMEM, pltpu.SemaphoreType.DMA
    results = (
        jax.ShapeDtypeStruct((3, width // n_sp, cols3 // 3), F32),
        jax.ShapeDtypeStruct((cols // n_sp, width), F32),
    )
    dw, dwo, g = pl.pallas_call(
        functools.partial(reduce_kernel, n_chip),
        out_shape=results + (jax.ShapeDtypeStruct((8, 128), F32),),
        in_specs=[spec] * 3,
        out_specs=(spec,) * 3,
        scratch_shapes=[
            vmem((n_chip,) + w_shape, F32), vmem((n_chip,) + o_shape, F32),
            vmem((n_chip,) + w_shape, F32), vmem((n_chip,) + o_shape, F32),
            vmem((2,) + w_half, F32), vmem((2,) + o_half, F32),
            vmem((2,) + w_shape, F32), vmem((2,) + o_shape, F32),
            vmem((2, 8, 128), F32), vmem((n_chip, 8, 128), F32),
            dma((3,)), dma((3,)), dma((n_chip,)), dma((n_chip,)), dma((6, 2)), dma((6, 2)),
        ],
        compiler_params=pltpu.CompilerParams(collective_id=1, has_side_effects=True),
        name="reduce",
    )(dw, dwo, dgb)
    row = jax.ShapeDtypeStruct((1, width), F32)
    return pl.pallas_call(
        finish_kernel,
        out_shape=results + (row, row, jax.ShapeDtypeStruct(grad_temp.shape, F32)),
        in_specs=[spec] * 3 + [smem],
        out_specs=(spec,) * 4 + (smem,),
        name="finish",
    )(dw, dwo, g, grad_temp)


def solution(mesh):
    n_tp, n_sp = mesh.shape["tp"], mesh.shape["sp"]
    row_spec = P(("dp", "sp"), None)

    def local_step(x, g, w_qkv, w_out, ln_gamma, ln_beta, temperature):
        width = x.shape[1]
        gamma, beta = ln_gamma.reshape(1, width), ln_beta.reshape(1, width)
        me_t = lax.axis_index("tp").astype(jnp.int32).reshape(1)
        w, wo, mats, rows, grad_temp = run_state(
            n_sp, n_tp, x, g, w_qkv.transpose(1, 0, 2), w_out, gamma, beta, temperature
        )
        y, dx, dw, dwo, dgb = run_main(n_tp, me_t, x, g, w, wo, mats, rows, gamma, beta)
        dw, dwo, dgamma, dbeta, grad_temp = run_reduce(n_sp, dw, dwo, dgb, grad_temp)
        return y, dx, dw.transpose(1, 0, 2), dwo, dgamma.reshape(-1), dbeta.reshape(-1), grad_temp

    in_specs = (row_spec, row_spec, P(None, None, "tp"), P("tp", None), P(None), P(None), P(None))
    out_specs = (row_spec, row_spec, P(("dp", "sp"), None, "tp"), P(("dp", "tp", "sp"), None), P("dp"), P("dp"), P("dp"))
    return jax.shard_map(local_step, mesh=mesh, in_specs=in_specs, out_specs=out_specs, check_vma=False)
```

time: 1410 us -> 190 us (0.13)
  waiting for transfers between devices: 1120 us -> 0 us
  Pallas kernels: 0 us -> 182 us
  matrix products: 123 us -> 0 us
  other arithmetic: 95.6 us -> 0 us
  local copies, waits for them, and re-layouts: 32.1 us -> 7.7 us
  blocking collectives: 23.7 us -> 0 us
    psum x2 -> x0, waiting for transfers between devices: 1120 us -> none  [the longest x1 1060 us: local_step(): lax.psum(y_part, 'tp')]
    pallas_call x0 -> x4, Pallas kernels: none -> 182 us  [the longest x1 114 us: run_main(): pl.pallas_call(functools.partial(main_kernel, n_tp), grid_spec=pltpu.Pref...]
    dot_general x11 -> x0, matrix products: 103 us -> none  [the longest x1 19.2 us: local_step(): jnp.einsum('nd,nec->dec', u_act, dqkv_act, preferred_element_type=jnp.flo...]
    convert_element_type x2 -> x0, other arithmetic: 54.7 us -> none  [the longest x1 44.3 us: local_step(): (grad_blk.astype(jnp.float32) + layer_norm_bwd(grad_u, x_hat, inv_std, ln...]
    reduce_sum x3 -> x0, other arithmetic: 36.5 us -> none  [the longest x1 22.2 us: local_step(): jnp.sum(grad_u * x_hat, axis=0)]
    unnamed x1 -> x0, matrix products: 20 us -> none
    another operation x3 -> x0, local copies, waits for them, and re-layouts: 19.1 us -> none  [local_step(): jnp.stack([dq_act, dk_act, dv_act], axis=1).reshape(tokens, 3, local_cols)]
  transfers between devices with their start and end apart: 4 -> 0, of which waited for: 2 -> 0; matrix products, arithmetic and copies ran while one was open for 7% -> 0% of each run, Pallas kernels for 0% -> 0%
where the time goes in v2:
time: 190 us
  Pallas kernels  182 us (96%)
  local copies, waits for them, and re-layouts  7.7 us (4%)
    pallas_call x1, Pallas kernels, run_main(): pl.pallas_call(functools.partial(main_kernel, n_tp), grid_spec=pltpu.Pref...  114 us
    pallas_call x1, Pallas kernels, run_state(): pl.pallas_call(functools.partial(state_kernel, n_sp, n_tp), grid=(tokens...  52.5 us
    pallas_call x1, Pallas kernels, run_reduce(): pl.pallas_call(functools.partial(reduce_kernel, n_chip), out_shape=result...  13.2 us
    unnamed x20, local copies, waits for them, and re-layouts  7.7 us

profile of v2, /device:TPU:97, one launch (start us, length us, event | category | flops | bytes accessed | tf_op | source)
XLA Modules:
  0.0 190.1 jit_solution(816075175260407246)
XLA Ops:
  0.6 0.0 copy-start
  0.6 1.0 copy-done
  1.6 0.0 copy-start.1
  1.6 0.9 copy-done.1
  2.5 0.0 copy-start.2
  2.5 0.7 copy-done.2
  3.2 0.0 copy-start.3
  3.2 0.7 copy-done.3
  3.9 0.0 copy-start.4
  3.9 0.7 copy-done.4
  4.6 52.5 %state.1 = (bf16[4,3,512,128]{3,2,1,0:T(8,128)(2,1)S(1)}, bf16[4,128,512]{2,1,0:T(8,128)(2,1)S(1)}, bf16[4,128,128]{2,1,0:T(8,128)(2,1)S(1)}, f32[4,8,128]{2,1,0:T(8,128)S(1)}, f32[8]{0:T(128)S(1)}) custom-call(bf16[16384,512]{1,0:T(8,128)(2,1)} %x_ref.3, bf16[16384,512]{1,0:T(8,128)(2,1)} %g_ref.3, bf16[3,512,128]{2,1,0:T(8,128)(2,1)S(1)} %bitcast.9, ...), custom_call_target="tpu_custom_call" | custom-call | tf_op jit(solution)/shard_map/state/pallas_call | solution.py:195
  57.0 0.0 copy-start.5
  57.0 0.6 copy-done.5
  57.6 0.0 copy-start.6
  57.6 1.2 copy-done.6
  58.8 0.0 copy-start.7
  58.8 0.8 copy-done.7
  59.6 0.0 copy-start.8
  59.6 0.6 copy-done.8
  60.2 0.0 copy-start.9
  60.2 0.6 copy-done.9
  60.8 114.3 %main.1 = (bf16[16384,512]{1,0:T(8,128)(2,1)}, bf16[16384,512]{1,0:T(8,128)(2,1)}, f32[512,384]{1,0:T(8,128)}, f32[128,512]{1,0:T(8,128)}, f32[8,512]{1,0:T(8,128)}) custom-call(s32[1]{0:T(128)} %bitcast.t_ref, bf16[16384,512]{1,0:T(8,128)(2,1)} %x_ref.3, bf16[16384,512]{1,0:T(8,128)(2,1)} %g_ref.3, bf16[4,3,512,128]{3,2,1,0:T(8,128)(2,1)} %copy-done.6, ...), custom_call_target="tpu_custom_call" | custom-call | flops 94489280512 | bytes 67108864 | tf_op jit(solution)/shard_map/main/pallas_call | solution.py:326
  175.2 13.2 %reduce.1 = (f32[3,64,128]{2,1,0:T(8,128)}, f32[16,512]{1,0:T(8,128)}, f32[8,128]{1,0:T(8,128)}) custom-call(f32[4,2,64,384]{3,2,1,0:T(8,128)} %bitcast.15, f32[4,2,16,512]{3,2,1,0:T(8,128)} %bitcast.16, f32[8,512]{1,0:T(8,128)} %get-tuple-element.33.dgb_ref), custom_call_target="tpu_custom_call" | custom-call | tf_op jit(solution)/shard_map/reduce/pallas_call | solution.py:452
  188.3 1.6 finish.1
Async XLA Ops:
  0.6 1.0 copy-start
  1.6 0.9 copy-start.1
  2.5 0.7 copy-start.2
  3.2 0.7 copy-start.3
  3.9 0.7 copy-start.4
  57.0 0.6 copy-start.5
  57.6 1.2 copy-start.6
  58.8 0.8 copy-start.7
  59.6 0.6 copy-start.8
  60.2 0.6 copy-start.9

commit v3 on v2

--- a/solution.py
+++ b/solution.py
@@ -13,6 +13,7 @@
 MESH = pl.DeviceIdType.MESH
 STATS_ROWS = 2048
 STATS_SUB = 512
+CHUNK = 128
 MAIN_ROWS = 2048
 MAIN_SUB = 512
 
@@ -23,6 +24,10 @@
 
 def dot_rows(lhs, rhs):
     return lax.dot_general(lhs, rhs, (((0,), (0,)), ((), ())), preferred_element_type=F32)
+
+
+def dot_cols(lhs, rhs):
+    return lax.dot_general(lhs, rhs, (((1,), (1,)), ((), ())), preferred_element_type=F32)
 
 
 def layer_norm(x, gamma, beta):
@@ -32,11 +37,19 @@
     return x_hat, inv_std, (x_hat * gamma + beta).astype(BF16)
 
 
+def weave(steps, *sides):
+    order = [((i + 0.5) / len(steps), 0, i, f) for i, f in enumerate(steps)]
+    for n, side in enumerate(sides):
+        order += [((i + 0.25) / len(side), n + 1, i, f) for i, f in enumerate(side)]
+    for *_, f in sorted(order, key=lambda e: e[:3]):
+        f()
+
+
 def state_kernel(
     n_sp, n_tp, x_ref, g_ref, w_ref, wo_ref, gamma_ref, beta_ref, temp_ref, w_any, wo_any,
     w_all, wo_all, mats_ref, rows_ref, gt_ref,
-    w_s, u_s, qk_s, dv_s, pair, gath, mats, rows,
-    w_send, w_recv, w_local, pair_send, pair_recv, sp_send, sp_recv, tp_send, tp_recv,
+    wt_s, wot_s, u_s, qk_s, vd_s, pair, gath, mats, rows,
+    w_send, w_recv, p_send, p_recv, w_local, pair_send, pair_recv, sp_send, sp_recv, tp_send, tp_recv,
 ):
     step = pl.program_id(0)
     me_s, me_t = lax.axis_index("sp"), lax.axis_index("tp")
@@ -48,15 +61,38 @@
     chips = [{"sp": 2 * lax.rem(chip + d, n_chip) + core} for d in range(n_chip)]
     tps = [{"tp": lax.rem(me_t + d, n_tp)} for d in range(n_tp)]
 
-    def weight_copies():
+    n_rows, n_wo = w_any.shape[1] // 2, wo_any.shape[0] // 2
+    rows_of = pl.ds(pl.multiple_of(core * n_rows, n_rows), n_rows)
+    wo_of = pl.ds(pl.multiple_of(core * n_wo, n_wo), n_wo)
+
+    def gather_copies():
+        copies = []
         for d in range(1, n_tp):
-            for k, (src, dst) in enumerate(((w_any, w_all), (wo_any, wo_all))):
-                yield pltpu.make_async_remote_copy(
-                    src_ref=src, dst_ref=dst.at[me_t], send_sem=w_send.at[k, d], recv_sem=w_recv.at[k, d],
+            for k, (src, dst) in enumerate(
+                ((w_any.at[:, rows_of], w_all.at[me_t, :, rows_of]), (wo_any.at[wo_of], wo_all.at[me_t, wo_of]))
+            ):
+                copies.append(pltpu.make_async_remote_copy(
+                    src_ref=src, dst_ref=dst, send_sem=w_send.at[k, d], recv_sem=w_recv.at[k, d],
                     device_id=tps[d], device_id_type=MESH,
-                )
-        for k, (src, dst) in enumerate(((w_any, w_all), (wo_any, wo_all))):
-            yield pltpu.make_async_copy(src, dst.at[me_t], w_local.at[k])
+                ))
+        return copies
+
+    def pass_copies():
+        copies = []
+        for d in range(1, n_tp):
+            t = lax.rem(me_t - d + n_tp, n_tp)
+            for k, ref in enumerate((w_all.at[t, :, rows_of], wo_all.at[t, wo_of])):
+                copies.append(pltpu.make_async_remote_copy(
+                    src_ref=ref, dst_ref=ref, send_sem=p_send.at[k, d], recv_sem=p_recv.at[k, d],
+                    device_id=partner, device_id_type=MESH,
+                ))
+        return copies
+
+    def local_copies():
+        return [
+            pltpu.make_async_copy(src, dst.at[me_t], w_local.at[k])
+            for k, (src, dst) in enumerate(((w_any, w_all), (wo_any, wo_all)))
+        ]
 
     @pl.when(step == 0)
     def _():
@@ -64,33 +100,42 @@
         for peer in [partner] + chips[1:] + tps[1:]:
             pl.semaphore_signal(barrier, inc=1, device_id=peer, device_id_type=MESH)
         pl.semaphore_wait(barrier, n_chip + n_tp - 1)
-        for copy in weight_copies():
+        for copy in gather_copies() + local_copies():
             copy.start()
         for e in range(3):
-            w_s[:, e * cols : (e + 1) * cols] = w_ref[e]
-        w_s[:, 3 * cols :] = wo_ref[...].T
+            wt_s[e * cols : (e + 1) * cols, :] = w_ref[e].T
+        wot_s[...] = wo_ref[...].T
         qk_s[...] = jnp.zeros_like(qk_s)
-        dv_s[...] = jnp.zeros_like(dv_s)
+        vd_s[...] = jnp.zeros_like(vd_s)
+
+    @pl.when(step == pl.num_programs(0) - 1)
+    def _():
+        for copy in gather_copies():
+            copy.wait()
+        for copy in pass_copies():
+            copy.start()
 
     sub = u_s.shape[1]
     n_sub = x_ref.shape[0] // sub
     gamma, beta = gamma_ref[...], beta_ref[...]
 
     def norm(s):
-        u_s[s % 2] = layer_norm(x_ref[s * sub : (s + 1) * sub].astype(F32), gamma, beta)[2]
+        def piece(at):
+            x = x_ref[s * sub + at : s * sub + at + CHUNK].astype(F32)
+            u_s[s % 2, at : at + CHUNK] = layer_norm(x, gamma, beta)[2]
+
+        return [functools.partial(piece, at) for at in range(0, sub, CHUNK)]
 
     def sums(s):
-        u = u_s[s % 2]
-        qk = dot(u, w_s[:, : 2 * cols]).astype(BF16)
-        v = dot(u, w_s[:, 2 * cols : 3 * cols]).astype(BF16)
-        dout = dot(g_ref[s * sub : (s + 1) * sub], w_s[:, 3 * cols :]).astype(BF16)
-        qk_s[...] += dot_rows(qk, qk)
-        dv_s[...] += dot_rows(dout, v)
-
-    norm(0)
+        qkv = dot_cols(wt_s[...], u_s[s % 2]).astype(BF16)
+        qk_s[...] += dot_cols(qkv[: 2 * cols], qkv[: 2 * cols])
+        dout = dot(g_ref[s * sub : (s + 1) * sub], wot_s[...]).astype(BF16)
+        vd_s[...] += dot(qkv[2 * cols :], dout)
+
+    weave(norm(0))
     for s in range(n_sub):
         if s + 1 < n_sub:
-            norm(s + 1)
+            weave(norm(s + 1))
         sums(s)
 
     @pl.when(step == pl.num_programs(0) - 1)
@@ -106,7 +151,7 @@
             return jnp.sum(jnp.where(eye, block, 0.0), axis=0, keepdims=True)
 
         pair[0, :hd] = fold(qk_s[:cols, cols:])
-        pair[0, hd : 2 * hd] = fold(dv_s[...])
+        pair[0, hd : 2 * hd] = fold(vd_s[...].T)
         pair[0, 2 * hd :] = jnp.concatenate(
             [diag_row(qk_s[:cols, :cols]), diag_row(qk_s[cols:, cols:]), jnp.zeros((6, cols), F32)], axis=0
         )
@@ -176,7 +221,7 @@
             rows_ref[t] = part
             gt_ref[2 * t] = part[2, 0]
             gt_ref[2 * t + 1] = part[2, hd]
-        for copy in weight_copies():
+        for copy in pass_copies() + local_copies():
             copy.wait()
 
 
@@ -205,15 +250,15 @@
         in_specs=[tile, tile, whole(w.shape), whole(wo.shape), whole((1, width)), whole((1, width)), smem, hbm, hbm],
         out_specs=(hbm, hbm, whole((n_tp, cols, cols)), whole((n_tp, 8, cols)), smem),
         scratch_shapes=[
-            vmem((width, 4 * cols), BF16), vmem((2, sub, width), BF16),
+            vmem((3 * cols, width), BF16), vmem((width, cols), BF16), vmem((2, sub, width), BF16),
             vmem((2 * cols, 2 * cols), F32), vmem((cols, cols), F32),
             vmem((2, cols + 8, cols), F32), vmem((n_sp // 2, cols + 8, cols), F32),
             vmem((n_tp, cols, cols), BF16), vmem((n_tp, 8, cols), F32),
-            dma((2, n_tp)), dma((2, n_tp)), dma((2,)), dma, dma, dma((n_sp // 2,)), dma((n_sp // 2,)),
+            dma((2, n_tp)), dma((2, n_tp)), dma((2, n_tp)), dma((2, n_tp)), dma((2,)), dma, dma, dma((n_sp // 2,)), dma((n_sp // 2,)),
             dma((2, n_tp)), dma((2, n_tp)),
         ],
         compiler_params=pltpu.CompilerParams(
-            dimension_semantics=("arbitrary",), vmem_limit_bytes=48 << 20, collective_id=0, has_side_effects=True
+            dimension_semantics=("arbitrary",), vmem_limit_bytes=60 << 20, collective_id=0, has_side_effects=True
         ),
         name="state",
     )(x, g, w, wo, gamma, beta, temp, w, wo)

time: 190 us -> 175 us (0.921)
  Pallas kernels: 182 us -> 174 us
  local copies, waits for them, and re-layouts: 7.7 us -> 0 us
    unnamed x20 -> x0, local copies, waits for them, and re-layouts: 7.7 us -> none
    pallas_call x1, Pallas kernels: 52.5 us -> 44.9 us  [run_state(): pl.pallas_call(functools.partial(state_kernel, n_sp, n_tp), grid=(tokens...]
where the time goes in v3:
time: 175 us
  Pallas kernels  174 us (99%)
    pallas_call x1, Pallas kernels, run_main(): pl.pallas_call(functools.partial(main_kernel, n_tp), grid_spec=pltpu.Pref...  115 us
    pallas_call x1, Pallas kernels, run_state(): pl.pallas_call(functools.partial(state_kernel, n_sp, n_tp), grid=(tokens...  44.9 us
    pallas_call x1, Pallas kernels, run_reduce(): pl.pallas_call(functools.partial(reduce_kernel, n_chip), out_shape=result...  13.2 us

profile of v3, /device:TPU:97, one launch (start us, length us, event | category | flops | bytes accessed | tf_op | source)
XLA Modules:
  0.0 175.0 jit_solution(1973724182689192280)
XLA Ops:
  0.6 44.9 %state.1 = (bf16[4,3,512,128]{3,2,1,0:T(8,128)(2,1)}, bf16[4,128,512]{2,1,0:T(8,128)(2,1)}, bf16[4,128,128]{2,1,0:T(8,128)(2,1)}, f32[4,8,128]{2,1,0:T(8,128)}, f32[8]{0:T(128)}) custom-call(bf16[16384,512]{1,0:T(8,128)(2,1)} %x_ref.3, bf16[16384,512]{1,0:T(8,128)(2,1)} %g_ref.3, bf16[3,512,128]{2,1,0:T(8,128)(2,1)} %bitcast.9, bf16[128,512]{1,0:T(8,128)(2,1)} %wo_any.1, ...), custom_call_target="tpu_custom_call" | custom-call | tf_op jit(solution)/shard_map/state/pallas_call | solution.py:240
  45.5 114.6 %main.1 = (bf16[16384,512]{1,0:T(8,128)(2,1)}, bf16[16384,512]{1,0:T(8,128)(2,1)}, f32[512,384]{1,0:T(8,128)}, f32[128,512]{1,0:T(8,128)}, f32[8,512]{1,0:T(8,128)}) custom-call(s32[1]{0:T(128)} %bitcast.t_ref, bf16[16384,512]{1,0:T(8,128)(2,1)} %x_ref.3, bf16[16384,512]{1,0:T(8,128)(2,1)} %g_ref.3, bf16[4,3,512,128]{3,2,1,0:T(8,128)(2,1)} %get-tuple-element.25.w_ref, ...), custom_call_target="tpu_custom_call" | custom-call | flops 94489280512 | bytes 67108864 | tf_op jit(solution)/shard_map/main/pallas_call | solution.py:371
  160.1 13.2 %reduce.1 = (f32[3,64,128]{2,1,0:T(8,128)}, f32[16,512]{1,0:T(8,128)}, f32[8,128]{1,0:T(8,128)}) custom-call(f32[4,2,64,384]{3,2,1,0:T(8,128)} %bitcast.11, f32[4,2,16,512]{3,2,1,0:T(8,128)} %bitcast.12, f32[8,512]{1,0:T(8,128)} %get-tuple-element.33.dgb_ref), custom_call_target="tpu_custom_call" | custom-call | tf_op jit(solution)/shard_map/reduce/pallas_call | solution.py:497
  173.3 1.6 finish.1

commit v4 on v3

--- a/solution.py
+++ b/solution.py
@@ -11,8 +11,8 @@
 F32 = jnp.float32
 BF16 = jnp.bfloat16
 MESH = pl.DeviceIdType.MESH
-STATS_ROWS = 2048
-STATS_SUB = 512
+STATS_ROWS = 4096
+STATS_SUB = 1024
 CHUNK = 128
 MAIN_ROWS = 2048
 MAIN_SUB = 512
@@ -48,7 +48,7 @@
 def state_kernel(
     n_sp, n_tp, x_ref, g_ref, w_ref, wo_ref, gamma_ref, beta_ref, temp_ref, w_any, wo_any,
     w_all, wo_all, mats_ref, rows_ref, gt_ref,
-    wt_s, wot_s, u_s, qk_s, vd_s, pair, gath, mats, rows,
+    wt_s, wot_s, u_s, qk_s, vd_s, pair, got, gath, mats, rows,
     w_send, w_recv, p_send, p_recv, w_local, pair_send, pair_recv, sp_send, sp_recv, tp_send, tp_recv,
 ):
     step = pl.program_id(0)
@@ -97,9 +97,10 @@
     @pl.when(step == 0)
     def _():
         barrier = pltpu.get_barrier_semaphore()
-        for peer in [partner] + chips[1:] + tps[1:]:
+        others = [{"tp": peer["tp"], "sp": partner["sp"]} for peer in tps[1:]]
+        for peer in [partner] + chips[1:] + tps[1:] + others:
             pl.semaphore_signal(barrier, inc=1, device_id=peer, device_id_type=MESH)
-        pl.semaphore_wait(barrier, n_chip + n_tp - 1)
+        pl.semaphore_wait(barrier, n_chip + 2 * n_tp - 2)
         for copy in gather_copies() + local_copies():
             copy.start()
         for e in range(3):
@@ -140,28 +141,29 @@
 
     @pl.when(step == pl.num_programs(0) - 1)
     def _():
-        lane = lax.broadcasted_iota(jnp.int32, (hd, cols), 1)
-        first = lane < hd
+        first = lax.broadcasted_iota(jnp.int32, (hd, cols), 1) < hd
         eye = lax.broadcasted_iota(jnp.int32, (cols, cols), 0) == lax.broadcasted_iota(jnp.int32, (cols, cols), 1)
-
-        def fold(block):
-            return jnp.where(first, block[:hd], block[hd:])
 
         def diag_row(block):
             return jnp.sum(jnp.where(eye, block, 0.0), axis=0, keepdims=True)
 
-        pair[0, :hd] = fold(qk_s[:cols, cols:])
-        pair[0, hd : 2 * hd] = fold(vd_s[...].T)
-        pair[0, 2 * hd :] = jnp.concatenate(
-            [diag_row(qk_s[:cols, :cols]), diag_row(qk_s[cols:, cols:]), jnp.zeros((6, cols), F32)], axis=0
-        )
+        gram, d_attn = qk_s[:cols, cols:], vd_s[...].T
+        q_row, k_row = diag_row(qk_s[:cols, :cols]), diag_row(qk_s[cols:, cols:])
+        for h in range(2):
+            g_h, d_h = gram[h * hd : (h + 1) * hd], d_attn[h * hd : (h + 1) * hd]
+            if h == 0:
+                top, low = jnp.where(first, g_h, pltpu.roll(d_h, hd, 1)), (q_row, pltpu.roll(jnp.broadcast_to(k_row, (8, cols)), hd, 1)[:1])
+            else:
+                top, low = jnp.where(first, pltpu.roll(g_h, hd, 1), d_h), (pltpu.roll(jnp.broadcast_to(q_row, (8, cols)), hd, 1)[:1], k_row)
+            pair[h, :hd] = top
+            pair[h, hd:] = jnp.broadcast_to(jnp.where(first[:1], low[0], low[1]), (8, cols))
         copy = pltpu.make_async_remote_copy(
-            src_ref=pair.at[0], dst_ref=pair.at[1], send_sem=pair_send, recv_sem=pair_recv,
+            src_ref=pair.at[1 - core], dst_ref=got, send_sem=pair_send, recv_sem=pair_recv,
             device_id=partner, device_id_type=MESH,
         )
         copy.start()
         copy.wait()
-        gath[0] = pair[0] + pair[1]
+        gath[0] = pair[core] + got[...]
         copies = []
         for d in range(1, n_chip):
             copy = pltpu.make_async_remote_copy(
@@ -176,51 +178,56 @@
         for c in range(1, n_chip):
             total = total + gath[lax.rem(chip - c + n_chip, n_chip)]
 
-        gram, d_attn = total[:hd], total[hd : 2 * hd]
-        q_row, k_row = total[2 * hd : 2 * hd + 1], total[2 * hd + 1 : 2 * hd + 2]
-        q_all = jnp.sum(jnp.where(eye, jnp.broadcast_to(q_row, (cols, cols)), 0.0), axis=1, keepdims=True)
-        q_col = jnp.where(first, jnp.broadcast_to(q_all[:hd], (hd, cols)), jnp.broadcast_to(q_all[hd:], (hd, cols)))
-        temp = jnp.where(first, temp_ref[2 * me_t], temp_ref[2 * me_t + 1])
-
-        def per_head(value, reduce, other):
-            lo = reduce(jnp.where(first, value, other), axis=1, keepdims=True)
-            hi = reduce(jnp.where(first, other, value), axis=1, keepdims=True)
-            return jnp.where(first, jnp.broadcast_to(lo, (hd, cols)), jnp.broadcast_to(hi, (hd, cols)))
-
+        gram, d_attn = total[:hd, :hd], total[:hd, hd:]
+        q_row, k_row = total[hd : hd + 1, :hd], total[hd : hd + 1, hd:]
+        same = lax.broadcasted_iota(jnp.int32, (hd, hd), 0) == lax.broadcasted_iota(jnp.int32, (hd, hd), 1)
+
+        def to_col(row):
+            return jnp.sum(jnp.where(same, jnp.broadcast_to(row, (hd, hd)), 0.0), axis=1, keepdims=True)
+
+        def to_row(col):
+            return jnp.sum(jnp.where(same, jnp.broadcast_to(col, (hd, hd)), 0.0), axis=0, keepdims=True)
+
+        q_col = to_col(q_row)
+        temp = temp_ref[2 * me_t + core]
         norm_prod = jnp.sqrt(q_col) * jnp.sqrt(k_row)
         gram_n = gram / norm_prod
         logit = temp * gram_n
-        expo = jnp.exp(logit - per_head(logit, jnp.max, -jnp.inf))
-        attn = expo / per_head(expo, jnp.sum, 0.0)
-        d_logit = attn * (d_attn - per_head(attn * d_attn, jnp.sum, 0.0))
-        temp_part = jnp.sum(per_head(d_logit * gram_n, jnp.sum, 0.0), axis=0, keepdims=True)
+        expo = jnp.exp(logit - jnp.max(logit, axis=1, keepdims=True))
+        attn = expo / jnp.sum(expo, axis=1, keepdims=True)
+        d_logit = attn * (d_attn - jnp.sum(attn * d_attn, axis=1, keepdims=True))
+        temp_part = jnp.sum(jnp.sum(d_logit * gram_n, axis=1, keepdims=True), axis=0, keepdims=True)
         grad_sn = temp * d_logit
         prod = grad_sn * gram_n
-        same = lax.broadcasted_iota(jnp.int32, (hd, cols), 0) == lax.rem(lane, hd)
-        q_coef = jnp.sum(jnp.where(same, -per_head(prod, jnp.sum, 0.0) / q_col, 0.0), axis=0, keepdims=True)
+        q_coef = to_row(-jnp.sum(prod, axis=1, keepdims=True) / q_col)
         k_coef = -jnp.sum(prod, axis=0, keepdims=True) / k_row
 
-        mats[0, :hd] = attn.astype(BF16)
-        mats[0, hd:] = (grad_sn / norm_prod).astype(BF16)
-        rows[0] = jnp.concatenate([q_coef, k_coef, temp_part, jnp.zeros((5, cols), F32)], axis=0)
+        mats[0] = jnp.concatenate([attn, grad_sn / norm_prod], axis=1).astype(BF16)
+        rows[0] = jnp.concatenate(
+            [jnp.concatenate([q_coef, k_coef], axis=1), jnp.broadcast_to(temp_part, (7, cols))], axis=0
+        )
         copies = []
-        for d in range(1, n_tp):
-            for k, ref in enumerate((mats, rows)):
-                copy = pltpu.make_async_remote_copy(
-                    src_ref=ref.at[0], dst_ref=ref.at[d], send_sem=tp_send.at[k, d], recv_sem=tp_recv.at[k, d],
-                    device_id=tps[d], device_id_type=MESH,
-                )
-                copy.start()
-                copies.append(copy)
+        for d in range(n_tp):
+            for j in range(2):
+                if d + j > 0:
+                    slot = 2 * d + j
+                    to = {"tp": lax.rem(me_t + d, n_tp), "sp": me_s + j * (1 - 2 * core)}
+                    for k, ref in enumerate((mats, rows)):
+                        copy = pltpu.make_async_remote_copy(
+                            src_ref=ref.at[0], dst_ref=ref.at[slot], send_sem=tp_send.at[k, slot],
+                            recv_sem=tp_recv.at[k, slot], device_id=to, device_id_type=MESH,
+                        )
+                        copy.start()
+                        copies.append(copy)
         for copy in copies:
             copy.wait()
         for t in range(n_tp):
-            slot = lax.rem(me_t - t + n_tp, n_tp)
-            mats_ref[t] = mats[slot]
-            part = rows[slot]
-            rows_ref[t] = part
-            gt_ref[2 * t] = part[2, 0]
-            gt_ref[2 * t + 1] = part[2, hd]
+            for c in range(2):
+                slot = 2 * lax.rem(me_t - t + n_tp, n_tp) + core + c - 2 * core * c
+                mats_ref[2 * t + c] = mats[slot]
+                part = rows[slot]
+                rows_ref[2 * t + c] = part
+                gt_ref[2 * t + c] = part[1, 0]
         for copy in pass_copies() + local_copies():
             copy.wait()
 
@@ -228,6 +235,7 @@
 def run_state(n_sp, n_tp, x, g, w, wo, gamma, beta, temp):
     tokens, width = x.shape
     cols = wo.shape[0]
+    hd = cols // 2
     r, sub = STATS_ROWS, STATS_SUB
     tile = pl.BlockSpec((r, width), lambda i: (i, 0))
 
@@ -243,19 +251,19 @@
         out_shape=(
             jax.ShapeDtypeStruct((n_tp,) + w.shape, BF16),
             jax.ShapeDtypeStruct((n_tp,) + wo.shape, BF16),
-            jax.ShapeDtypeStruct((n_tp, cols, cols), BF16),
-            jax.ShapeDtypeStruct((n_tp, 8, cols), F32),
+            jax.ShapeDtypeStruct((2 * n_tp, hd, cols), BF16),
+            jax.ShapeDtypeStruct((2 * n_tp, 8, cols), F32),
             jax.ShapeDtypeStruct(temp.shape, F32),
         ),
         in_specs=[tile, tile, whole(w.shape), whole(wo.shape), whole((1, width)), whole((1, width)), smem, hbm, hbm],
-        out_specs=(hbm, hbm, whole((n_tp, cols, cols)), whole((n_tp, 8, cols)), smem),
+        out_specs=(hbm, hbm, whole((2 * n_tp, hd, cols)), whole((2 * n_tp, 8, cols)), smem),
         scratch_shapes=[
             vmem((3 * cols, width), BF16), vmem((width, cols), BF16), vmem((2, sub, width), BF16),
             vmem((2 * cols, 2 * cols), F32), vmem((cols, cols), F32),
-            vmem((2, cols + 8, cols), F32), vmem((n_sp // 2, cols + 8, cols), F32),
-            vmem((n_tp, cols, cols), BF16), vmem((n_tp, 8, cols), F32),
+            vmem((2, hd + 8, cols), F32), vmem((hd + 8, cols), F32), vmem((n_sp // 2, hd + 8, cols), F32),
+            vmem((2 * n_tp, hd, cols), BF16), vmem((2 * n_tp, 8, cols), F32),
             dma((2, n_tp)), dma((2, n_tp)), dma((2, n_tp)), dma((2, n_tp)), dma((2,)), dma, dma, dma((n_sp // 2,)), dma((n_sp // 2,)),
-            dma((2, n_tp)), dma((2, n_tp)),
+            dma((2, 2 * n_tp)), dma((2, 2 * n_tp)),
         ],
         compiler_params=pltpu.CompilerParams(
             dimension_semantics=("arbitrary",), vmem_limit_bytes=60 << 20, collective_id=0, has_side_effects=True
@@ -289,13 +297,18 @@
         first = lax.broadcasted_iota(jnp.int32, (hd, cols), 1) < hd
         for t in range(n_tp):
             p, off = t // 2, (t % 2) * cols
-            for k, (plain, trans) in enumerate(((a_s, at_s), (g_s, gt_s))):
-                block = mats_ref[t, k * hd : (k + 1) * hd].astype(F32)
-                full = jnp.concatenate([jnp.where(first, block, 0.0), jnp.where(first, 0.0, block)], axis=0)
+            even, odd = mats_ref[2 * t].astype(F32), mats_ref[2 * t + 1].astype(F32)
+            for plain, trans, hi, lo in (
+                (a_s, at_s, even, pltpu.roll(odd, hd, 1)), (g_s, gt_s, pltpu.roll(even, hd, 1), odd)
+            ):
+                full = jnp.concatenate([jnp.where(first, hi, 0.0), jnp.where(first, 0.0, lo)], axis=0)
                 plain[p, off : off + cols, off : off + cols] = full.astype(BF16)
                 trans[p, off : off + cols, off : off + cols] = full.T.astype(BF16)
-            co_s[0:1, t * cols : (t + 1) * cols] = rows_ref[t, 0:1]
-            co_s[1:2, t * cols : (t + 1) * cols] = rows_ref[t, 1:2]
+            pair = [rows_ref[2 * t, 0:1], rows_ref[2 * t + 1, 0:1]]
+            turned = [pltpu.roll(jnp.broadcast_to(row, (8, cols)), hd, 1)[:1] for row in pair]
+            at = slice(t * cols, (t + 1) * cols)
+            co_s[0:1, at] = jnp.where(first[:1], pair[0], turned[1])
+            co_s[1:2, at] = jnp.where(first[:1], turned[0], pair[1])
         dwt_s[...] = jnp.zeros_like(dwt_s)
         dwo_ref[...] = jnp.zeros_like(dwo_ref)
         dgb_ref[...] = jnp.zeros_like(dgb_ref)
@@ -402,9 +415,9 @@
 
 
 def reduce_kernel(
-    n_chip, dw_ref, dwo_ref, dgb_ref, dw_out, dwo_out, g_out,
-    got_w, got_o, sum_w, sum_o, via_w, via_o, in_w, in_o, gam, in_g,
-    a_send, a_recv, g_send, g_recv, b_send, b_recv,
+    n_chip, dw_any, dwo_any, dgb_ref, dw_out, dwo_out, g_out,
+    dw_ref, dwo_ref, got_w, got_o, sum_w, sum_o, via_w, via_o, in_w, in_o, gam, in_g,
+    l_sem, a_send, a_recv, g_send, g_recv, b_send, b_recv,
 ):
     me = lax.axis_index("sp")
     core, chip = lax.rem(me, 2), me // 2
@@ -414,9 +427,17 @@
     barrier = pltpu.get_barrier_semaphore()
     for peer in [partner] + peers[1:]:
         pl.semaphore_signal(barrier, inc=1, device_id=peer, device_id_type=MESH)
+    loads = [
+        pltpu.make_async_copy(src, dst, l_sem.at[k])
+        for k, (src, dst) in enumerate(((dw_any, dw_ref), (dwo_any, dwo_ref)))
+    ]
+    for copy in loads:
+        copy.start()
     for c in range(4):
         gam[0, c : c + 1] = dgb_ref[0:1, c * 128 : (c + 1) * 128]
         gam[0, 4 + c : 5 + c] = dgb_ref[1:2, c * 128 : (c + 1) * 128]
+    for copy in loads:
+        copy.wait()
     pl.semaphore_wait(barrier, n_chip)
 
     def remote(src, dst, send, recv, peer):
@@ -426,13 +447,23 @@
         copy.start()
         return copy
 
-    w_copy = remote(dw_ref.at[:, 1 - core], got_w, a_send.at[0], a_recv.at[0], partner)
-    o_copy = remote(dwo_ref.at[:, 1 - core], got_o, a_send.at[1], a_recv.at[1], partner)
-    g_copy = remote(gam.at[0], gam.at[1], a_send.at[2], a_recv.at[2], partner)
-    w_copy.wait()
-    o_copy.wait()
-    sum_w[...] = dw_ref[:, core] + got_w[...]
-    sum_o[...] = dwo_ref[:, core] + got_o[...]
+    order = (far, right, left, chip)
+    halves = []
+    for i, c in enumerate(order):
+        halves.append((
+            remote(dw_ref.at[c, 1 - core], got_w.at[c], a_send.at[0, i], a_recv.at[0, i], partner),
+            remote(dwo_ref.at[c, 1 - core], got_o.at[c], a_send.at[1, i], a_recv.at[1, i], partner),
+        ))
+    g_copy = remote(gam.at[0], gam.at[1], a_send.at[2, 0], a_recv.at[2, 0], partner)
+
+    def join(i):
+        c = order[i]
+        for copy in halves[i]:
+            copy.wait()
+        sum_w[c] = dw_ref[c, core] + got_w[c]
+        sum_o[c] = dwo_ref[c, core] + got_o[c]
+
+    join(0)
     hw, ho = sum_w.shape[1] // 2, sum_o.shape[1] // 2
     w_half, o_half = (pl.ds(0, hw), pl.ds(hw, hw)), (pl.ds(0, ho), pl.ds(ho, ho))
 
@@ -440,10 +471,13 @@
     for h, peer in ((0, peers[1]), (1, peers[3])):
         via.append(remote(sum_w.at[far, w_half[h]], via_w.at[h], b_send.at[0, h], b_recv.at[0, h], peer))
         via.append(remote(sum_o.at[far, o_half[h]], via_o.at[h], b_send.at[1, h], b_recv.at[1, h], peer))
+    join(1)
+    join(2)
     for h, to, peer in ((0, right, peers[1]), (1, left, peers[3])):
         o = 1 - h
         near.append(remote(sum_w.at[to, w_half[o]], in_w.at[h, w_half[o]], b_send.at[2, h], b_recv.at[2, h], peer))
         near.append(remote(sum_o.at[to, o_half[o]], in_o.at[h, o_half[o]], b_send.at[3, h], b_recv.at[3, h], peer))
+    join(3)
     g_copy.wait()
     in_g[0] = gam[0] + gam[1]
     for d in range(1, n_chip):
@@ -497,15 +531,16 @@
     dw, dwo, g = pl.pallas_call(
         functools.partial(reduce_kernel, n_chip),
         out_shape=results + (jax.ShapeDtypeStruct((8, 128), F32),),
-        in_specs=[spec] * 3,
+        in_specs=[pl.BlockSpec(memory_space=pl.ANY)] * 2 + [spec],
         out_specs=(spec,) * 3,
         scratch_shapes=[
+            vmem(dw.shape, F32), vmem(dwo.shape, F32),
             vmem((n_chip,) + w_shape, F32), vmem((n_chip,) + o_shape, F32),
             vmem((n_chip,) + w_shape, F32), vmem((n_chip,) + o_shape, F32),
             vmem((2,) + w_half, F32), vmem((2,) + o_half, F32),
             vmem((2,) + w_shape, F32), vmem((2,) + o_shape, F32),
             vmem((2, 8, 128), F32), vmem((n_chip, 8, 128), F32),
-            dma((3,)), dma((3,)), dma((n_chip,)), dma((n_chip,)), dma((6, 2)), dma((6, 2)),
+            dma((2,)), dma((3, n_chip)), dma((3, n_chip)), dma((n_chip,)), dma((n_chip,)), dma((6, 2)), dma((6, 2)),
         ],
         compiler_params=pltpu.CompilerParams(collective_id=1, has_side_effects=True),
         name="reduce",

time: 175 us -> 170 us (0.971)
  Pallas kernels: 174 us -> 169 us
    pallas_call x1, Pallas kernels: 44.9 us -> 42.4 us  [run_state(): pl.pallas_call(functools.partial(state_kernel, n_sp, n_tp), grid=(tokens...]
    pallas_call x1, Pallas kernels: 13.2 us -> 10.8 us  [run_reduce(): pl.pallas_call(functools.partial(reduce_kernel, n_chip), out_shape=result...]
where the time goes in v4:
time: 170 us
  Pallas kernels  169 us (99%)
    pallas_call x1, Pallas kernels, run_main(): pl.pallas_call(functools.partial(main_kernel, n_tp), grid_spec=pltpu.Pref...  115 us
    pallas_call x1, Pallas kernels, run_state(): pl.pallas_call(functools.partial(state_kernel, n_sp, n_tp), grid=(tokens...  42.4 us
    pallas_call x1, Pallas kernels, run_reduce(): pl.pallas_call(functools.partial(reduce_kernel, n_chip), out_shape=result...  10.8 us

profile of v4, /device:TPU:97, one launch (start us, length us, event | category | flops | bytes accessed | tf_op | source)
XLA Modules:
  0.0 170.2 jit_solution(12076828190872327496)
XLA Ops:
  0.6 42.4 %state.1 = (bf16[4,3,512,128]{3,2,1,0:T(8,128)(2,1)}, bf16[4,128,512]{2,1,0:T(8,128)(2,1)}, bf16[8,64,128]{2,1,0:T(8,128)(2,1)}, f32[8,8,128]{2,1,0:T(8,128)}, f32[8]{0:T(128)}) custom-call(bf16[16384,512]{1,0:T(8,128)(2,1)} %x_ref.3, bf16[16384,512]{1,0:T(8,128)(2,1)} %g_ref.3, bf16[3,512,128]{2,1,0:T(8,128)(2,1)} %bitcast.9, bf16[128,512]{1,0:T(8,128)(2,1)} %wo_any.1, ...), custom_call_target="tpu_custom_call" | custom-call | tf_op jit(solution)/shard_map/state/pallas_call | solution.py:248
  43.1 114.6 %main.1 = (bf16[16384,512]{1,0:T(8,128)(2,1)}, bf16[16384,512]{1,0:T(8,128)(2,1)}, f32[512,384]{1,0:T(8,128)}, f32[128,512]{1,0:T(8,128)}, f32[8,512]{1,0:T(8,128)}) custom-call(s32[1]{0:T(128)} %bitcast.t_ref, bf16[16384,512]{1,0:T(8,128)(2,1)} %x_ref.3, bf16[16384,512]{1,0:T(8,128)(2,1)} %g_ref.3, bf16[4,3,512,128]{3,2,1,0:T(8,128)(2,1)} %get-tuple-element.25.w_ref, ...), custom_call_target="tpu_custom_call" | custom-call | flops 94489280512 | bytes 67108864 | tf_op jit(solution)/shard_map/main/pallas_call | solution.py:384
  157.7 10.8 %reduce.1 = (f32[3,64,128]{2,1,0:T(8,128)}, f32[16,512]{1,0:T(8,128)}, f32[8,128]{1,0:T(8,128)}) custom-call(f32[4,2,64,384]{3,2,1,0:T(8,128)} %bitcast.11, f32[4,2,16,512]{3,2,1,0:T(8,128)} %bitcast.12, f32[8,512]{1,0:T(8,128)} %get-tuple-element.33.dgb_ref), custom_call_target="tpu_custom_call" | custom-call | tf_op jit(solution)/shard_map/reduce/pallas_call | solution.py:531
  168.5 1.6 finish.1
